TPU v7x, 128 devices: a whole 4x4x4 slice. The times are simulated.
128 devices in a mesh: group: 4 (over y), member: 32 (over x, z, core).
Axes of the slice: x: 4, y: 4, z: 4, core: 2. Of those that a mesh axis runs over, the one named last changes fastest.
Arguments:
- samples: bfloat16 [65536, 768], P(('group', 'member')), may hold values from -6 to 6
- cell_of_row: int32 [65536, 1], P(('group', 'member')), may hold values from 0 to 511; in each aligned block of 512 rows (0 to 511, 512 to 1023, ...) at most 2 rows name the same one
- fine_centroids: bfloat16 [131072, 768], P(('group', 'member')), may hold values from -6 to 6
- sharpness: float32 [512], P(('group', 'member')), may hold values from 0.5 to 4
- mid_of_fine: int32 [131072], P(('group', 'member')), may hold values from 0 to 8191, as said below
- mid_centroids: float32 [8192, 768], P(('group', 'member')), may hold values from -6 to 6
- coarse_of_mid: int32 [8192], P(('group', 'member')), may hold values from 0 to 63
- coarse_centroids: float32 [64, 768], replicated, may hold values from -6 to 6
Outputs:
- fine_new: float32 [131072, 768], P(('group', 'member'))
- mids_new: float32 [8192, 768], P(('group', 'member'))
- coarse_new: float32 [64, 768], replicated
- reconstruction: bfloat16 [65536, 768], P(('group', 'member'))
Inputs may be any that keep to these rules, and one draw needn't show every extreme that they name: `cell_of_row`: among the rows of one device, no cell is named by more than 2 rows. `mid_of_fine`: fine centroid k's mid centroid lies in [g * 2048, (g + 1) * 2048) with g = k * 4 / 131072 rounded down.
All inputs are finite; a program needn't handle non-finite values.
Results may differ from a plain program's by a relative error of at most 0.007.
Values may be sent and summed in bfloat16 or wider, within the bound.
A program may use at most 64 MiB of HBM per device.

v0:
```python
import math

import jax
import jax.numpy as jnp
from jax import lax
from jax.sharding import Mesh
from jax.sharding import PartitionSpec as P

MEMBER = ("member_0", "member_1", "member_2")
GROUP_MEMBER = ("group", "member_0", "member_1", "member_2")


def split_up(array, dim, devices):
    dims = array.shape
    pieces = array.reshape(*dims[:dim], devices, dims[dim] // devices, *dims[dim + 1 :])
    return jnp.moveaxis(pieces, dim, 0)


def sent_and_summed(array, axis, dim):
    pieces = split_up(array, dim, lax.axis_size(axis))
    arrived = lax.all_to_all(pieces, axis, split_axis=0, concat_axis=0, tiled=True)
    return arrived.astype(jnp.float32).sum(axis=0)


def sum_in_two_steps(array, axes, dim):
    far, near = axes
    pieces = split_up(array, dim, lax.axis_size(far))
    nearer = sent_and_summed(pieces, near, dim + 1)
    arrived = lax.all_to_all(
        nearer.astype(jnp.bfloat16), far, split_axis=0, concat_axis=0, tiled=True
    )
    return arrived.astype(jnp.float32).sum(axis=0)


def sent_together(arrays, axis, dim, along):
    columns = [a.reshape(*a.shape[:along], -1) for a in arrays]
    both = jnp.concatenate(columns, axis=along)
    result, at, finished = (sum_in_two_steps(both, axis, dim), 0, [])
    for a, column in zip(arrays, columns):
        piece = result[..., at : at + column.shape[along]]
        finished.append(piece.reshape(*piece.shape[:along], *a.shape[along:]))
        at += column.shape[along]
    return tuple(finished)


def filled_up(lines, devices):
    spare = -len(lines) % devices
    return jnp.pad(lines, [(0, spare)] + [(0, 0)] * (lines.ndim - 1))


def copy_for_each(array, axis):
    copies = jnp.broadcast_to(array, (lax.axis_size(axis), *array.shape))
    return lax.all_to_all(copies, axis, split_axis=0, concat_axis=0, tiled=True)


def in_order(pieces, dim):
    pieces = jnp.moveaxis(pieces, 0, dim)
    dims = pieces.shape
    return pieces.reshape(*dims[:dim], dims[dim] * dims[dim + 1], *dims[dim + 2 :])


def gathered_by_axis(array, axes, dim):
    far, near = axes
    pieces = copy_for_each(copy_for_each(array, far), near)
    return in_order(pieces.swapaxes(0, 1).reshape(-1, *array.shape), dim)


def sum_at_owner(array, axis, dim):
    pieces = split_up(array, dim, lax.axis_size(axis))
    arrived = lax.all_to_all(pieces, axis, split_axis=0, concat_axis=0, tiled=True)
    return arrived.sum(axis=0)


def sum_in_two_steps_2(array, axes, dim):
    far, near = axes
    own = sum_at_owner(split_up(array, dim, lax.axis_size(far)), near, dim + 1)
    return jnp.sum(lax.all_to_all(own, far, 0, 0, tiled=True), axis=0)


def sum_by_parts(array, axes):
    padded = filled_up(array, lax.axis_size(axes[0]) * lax.axis_size(axes[1]))
    whole = gathered_by_axis(sum_in_two_steps_2(padded, axes, 0), axes, 0)
    return lax.slice_in_dim(whole, 0, len(array)).reshape(array.shape)


def in_one(arrays, axis):
    ends = [0]
    for a in arrays:
        ends.append(ends[-1] + a.size)
    running = sum_by_parts(jnp.concatenate([a.ravel() for a in arrays]), axis)
    return tuple((running[b:e].reshape(a.shape) for a, b, e in zip(arrays, ends, ends[1:])))


def shards(
    samples,
    cell_of_row,
    fine_centroids,
    sharpness,
    mid_of_fine,
    mid_centroids,
    coarse_of_mid,
    coarse_centroids,
):
    groups = lax.axis_size("group")
    members = lax.axis_size(MEMBER)
    devices = groups * members
    row_count = samples.shape[0]
    feature_width = samples.shape[1]
    cell_dev = sharpness.shape[0]
    fine_count = fine_centroids.shape[0] // cell_dev
    most_rows = 2 * row_count // (cell_dev * devices)
    total_cells = cell_dev * devices
    cell_ids = cell_of_row[:, 0]
    is_member = cell_ids[:, None] == jnp.arange(total_cells, dtype=jnp.int32)[None, :]
    one_hot = is_member.astype(jnp.bfloat16)
    lower_mask = (jnp.arange(row_count)[:, None] > jnp.arange(row_count)[None, :]).astype(
        jnp.bfloat16
    )
    earlier = jnp.dot(lower_mask, one_hot, preferred_element_type=jnp.float32)
    rank_in_cell = jnp.sum(earlier * is_member.astype(jnp.float32), axis=1).astype(jnp.int32)
    slot_index = cell_ids * most_rows + rank_in_cell
    outgoing = (
        jnp.zeros((total_cells * most_rows, feature_width), jnp.bfloat16)
        .at[slot_index]
        .set(samples)
    )
    outgoing = outgoing.reshape(devices, cell_dev * most_rows, feature_width)
    sent_counts = jnp.sum(is_member.astype(jnp.int32), axis=0).reshape(devices, cell_dev)
    arrived, arrived_counts = (
        lax.all_to_all(outgoing, GROUP_MEMBER, split_axis=0, concat_axis=0, tiled=True),
        lax.all_to_all(sent_counts, GROUP_MEMBER, split_axis=0, concat_axis=0, tiled=True),
    )
    arrived = arrived.reshape(devices, cell_dev, most_rows, feature_width)
    fine_local = fine_centroids.reshape(cell_dev, fine_count, feature_width)
    is_valid = jnp.arange(most_rows)[None, None, :] < arrived_counts[:, :, None]
    products = jnp.einsum("slmd,lkd->slmk", arrived, fine_local, preferred_element_type=jnp.float32)
    fine_float = fine_local.astype(jnp.float32)
    norms = jnp.sum(jnp.square(fine_float), axis=2)
    scores = (
        sharpness[None, :, None, None]
        * (products - 0.5 * norms[None, :, None, :])
        / math.sqrt(feature_width)
    )
    highest = jnp.max(scores, axis=3, keepdims=True)
    exponent = jnp.exp(scores - highest)
    probs = exponent / jnp.sum(exponent, axis=3, keepdims=True)
    resp = jnp.where(is_valid[..., None], probs, 0.0).astype(jnp.bfloat16)
    weighted = jnp.einsum("slmk,slmd->lkd", resp, arrived, preferred_element_type=jnp.float32)
    mass_total = jnp.sum(resp.astype(jnp.float32), axis=(0, 2))
    fine_new = (weighted + fine_float) / (mass_total[..., None] + 1.0)
    rebuilt = jnp.einsum(
        "slmk,lkd->slmd", resp, fine_local, preferred_element_type=jnp.float32
    ).astype(jnp.bfloat16)
    rebuilt = rebuilt.reshape(devices, cell_dev * most_rows, feature_width)
    returned = lax.all_to_all(rebuilt, GROUP_MEMBER, split_axis=0, concat_axis=0, tiled=True)
    reconstruction = returned.reshape(total_cells * most_rows, feature_width)[slot_index]
    group_index = lax.axis_index("group")
    mid_dev = mid_centroids.shape[0]
    mid_group = mid_dev * members
    local_mid = mid_of_fine - group_index * mid_group
    picker = (local_mid[:, None] == jnp.arange(mid_group, dtype=jnp.int32)[None, :]).astype(
        jnp.float32
    )
    weighted_flat = weighted.reshape(cell_dev * fine_count, feature_width)
    mass_flat = mass_total.reshape(cell_dev * fine_count)
    mid_part = jnp.dot(picker.T, weighted_flat, precision=lax.Precision.HIGHEST)
    mid_part_counts = jnp.sum(picker * mass_flat[:, None], axis=0)
    own_sum, own_count = sent_together(
        (mid_part.astype(jnp.bfloat16), mid_part_counts.astype(jnp.bfloat16)),
        (("member_0", "member_1"), "member_2"),
        0,
        1,
    )
    mids_new = (own_sum + mid_centroids) / (own_count[:, None] + 1.0)
    coarse_total = coarse_centroids.shape[0]
    coarse_route = (
        coarse_of_mid[:, None] == jnp.arange(coarse_total, dtype=jnp.int32)[None, :]
    ).astype(jnp.float32)
    coarse_part = jnp.dot(coarse_route.T, own_sum, precision=lax.Precision.HIGHEST)
    coarse_part_counts = jnp.sum(coarse_route * own_count[:, None], axis=0)
    coarse_sums, coarse_counts = in_one(
        (coarse_part, coarse_part_counts), (("group", "member_0", "member_1"), "member_2")
    )
    coarse_new = (coarse_sums + coarse_centroids) / (coarse_counts[:, None] + 1.0)
    return (
        fine_new.reshape(cell_dev * fine_count, feature_width),
        mids_new,
        coarse_new,
        reconstruction,
    )


def solution(mesh):
    split = Mesh(
        mesh.devices.reshape(mesh.shape["group"], 4, 4, 2),
        ("group", "member_0", "member_1", "member_2"),
    )
    placed = (
        P(GROUP_MEMBER, None),
        P(GROUP_MEMBER, None),
        P(GROUP_MEMBER, None),
        P(GROUP_MEMBER),
        P(GROUP_MEMBER),
        P(GROUP_MEMBER, None),
        P(GROUP_MEMBER),
        P(),
    )
    return jax.shard_map(
        shards,
        mesh=split,
        in_specs=placed,
        out_specs=(P(GROUP_MEMBER, None), P(GROUP_MEMBER, None), P(), P(GROUP_MEMBER, None)),
        check_vma=False,
    )
```

profile of v0, /device:TPU:1, one launch (start us, length us, event | category | flops | bytes accessed | tf_op | source)
XLA Modules:
  0.0 188.4 jit_solution(5756503327850326288)
XLA Ops:
  0.6 0.9 convert_reduce_fusion.2
  1.5 0.7 all_to_all.36
  2.2 11.5 %all-to-all-start = ((s32[128,1,4]{2,1,0:T(1,128)}), s32[128,1,4]{2,1,0:T(1,128)S(1)}, u32[]{:S(2)}, u32[]{:S(2)}) async-start(s32[128,1,4]{2,1,0:T(1,128)} %bitcast.1), calls=%async_computation | async-start | bytes 131072 | tf_op jit(solution)/shard_map/all_to_all | solution.py:131
  13.7 0.0 copy-start
  13.7 1.3 fusion.10
  15.1 0.7 compare_select_fusion
  15.8 0.0 copy-start.5
  15.8 4.4 %scatter_custom_fusion = bf16[1024,768]{1,0:T(8,128)(2,1)} fusion(s32[512]{0:T(512)S(1)} %bitcast.58, bf16[512,768]{1,0:T(8,128)(2,1)} %param.8, bf16[]{:T(256)} %constant.13.clone.1), kind=kCustom, calls=%fused_computation.27 | custom fusion | bytes 1573376 | tf_op jit(solution)/shard_map/scatter | solution.py:125
  20.1 3.0 %all-to-all-done = s32[128,1,4]{2,1,0:T(1,128)S(1)} async-done(((s32[128,1,4]{2,1,0:T(1,128)}), s32[128,1,4]{2,1,0:T(1,128)S(1)}, u32[]{:S(2)}, u32[]{:S(2)}) %all-to-all-start) | async-done | bytes 2080 | tf_op jit(solution)/shard_map/all_to_all | solution.py:131
  23.1 6.8 %all-to-all-start.1 = ((bf16[128,8,768]{2,1,0:T(8,128)(2,1)}), bf16[128,8,768]{2,1,0:T(8,128)(2,1)S(1)}, u32[]{:S(2)}, u32[]{:S(2)}) async-start(bf16[128,8,768]{2,1,0:T(8,128)(2,1)} %bitcast.5), calls=%async_computation.1 | async-start | bytes 3145728 | tf_op jit(solution)/shard_map/all_to_all | solution.py:130
  29.9 0.0 copy-start.7
  29.9 0.0 copy-done
  29.9 0.4 multiply_reduce_fusion
  30.3 0.0 copy-done.5
  30.4 0.1 copy.37
  30.4 24.0 %all-to-all-done.1 = bf16[128,8,768]{2,1,0:T(8,128)(2,1)S(1)} async-done(((bf16[128,8,768]{2,1,0:T(8,128)(2,1)}), bf16[128,8,768]{2,1,0:T(8,128)(2,1)S(1)}, u32[]{:S(2)}, u32[]{:S(2)}) %all-to-all-start.1) | async-done | bytes 1572896 | tf_op jit(solution)/shard_map/all_to_all | solution.py:130
  54.4 1.4 copy.38
  55.9 0.0 copy-done.7
  55.9 2.2 %fusion.17 = (f32[128,4,2]{0,2,1:T(2,128)S(1)}, f32[128,4,2,256]{3,0,2,1:T(8,128)S(1)}) fusion(bf16[128,4,2,768]{3,0,2,1:T(8,128)(2,1)} %bitcast.51, bf16[4,256,768,1]{2,1,3,0:T(8,128)(2,1)S(1)} %bitcast.46, f32[4,256]{1,0:T(4,128)S(1)} %mul.62, f32[4]{0:T(128)S(1)} %copy-done.7), kind=kOutput, calls=%fused_computation.49 | convolution fusion | flops 403964160 | bytes 4202512 | tf_op jit(solution)/shard_map/sub | solution.py:145
  58.1 0.4 convert_reduce_fusion.1
  58.5 0.0 copy-start.1
  58.5 1.2 select_reduce_fusion
  59.8 0.1 convert_element_type.72
  59.8 0.3 copy.41
  60.2 3.8 %fusion.4 = (f32[4,256,768]{2,1,0:T(8,128)}, f32[4,256,768,1]{2,1,3,0:T(8,128)S(1)}) fusion(bf16[4,256,768]{2,1,0:T(8,128)(2,1)S(1)} %bitcast.47, f32[4,256]{1,0:T(4,128)S(1)} %broadcast_add_fusion, bf16[128,4,2,256]{3,0,2,1:T(8,128)(2,1)S(1)} %get-tuple-element.7, bf16[128,4,2,768]{3,0,2,1:T(8,128)(2,1)} %bitcast.52), kind=kOutput, calls=%fused_computation.11 | convolution fusion | flops 405012480 | bytes 9965568 | tf_op jit(solution)/shard_map/slmk,slmd->lkd/dot_general | solution.py:148
  63.9 0.0 copy-done.1
  63.9 12.3 %fusion.3 = bf16[2048,768]{1,0:T(8,128)(2,1)S(1)} fusion(f32[1024,768]{1,0:T(8,128)S(1)} %bitcast.65, s32[1024]{0:T(1024)S(1)} %broadcast_subtract_fusion), kind=kOutput, calls=%fused_computation.9 | convolution fusion | flops 19331022848 | bytes 6295552 | tf_op jit(solution)/shard_map/dot_general | solution.py:166
  76.3 0.5 maximum_bitcast_fusion
  76.8 8.7 %all_to_all.57 = bf16[2,16,64,769]{3,2,1,0:T(8,128)(2,1)} all-to-all(bf16[2,16,64,769]{3,2,1,0:T(8,128)(2,1)S(1)} %maximum_bitcast_fusion), channel_id=1, replica_groups=mesh['group'=4,'member_0'=4,'member_1'=4,'member_2'=2] {'member_2'}, dimensions={0} | all-to-all | bytes 6299648 | tf_op jit(solution)/shard_map/all_to_all | solution.py:21
  85.5 3.0 %reduce_sum.108 = bf16[16,64,769]{2,1,0:T(8,128)(2,1)S(1)} reduce(bf16[2,16,64,769]{3,2,1,0:T(8,128)(2,1)} %all_to_all.57, bf16[]{:T(256)} %constant.13.clone.1), dimensions={0}, to_apply=%region_8.9 | reduce | flops 787456 | bytes 4724738 | tf_op jit(solution)/shard_map/reduce_sum | solution.py:22
  88.4 0.0 copy-start.6
  88.5 27.2 %all_to_all.58 = bf16[16,64,769]{2,1,0:T(8,128)(2,1)S(1)} all-to-all(bf16[16,64,769]{2,1,0:T(8,128)(2,1)S(1)} %reduce_sum.108), channel_id=1, replica_groups=mesh['group'=4,'member_0'=4,'member_1'=4,'member_2'=2] {'member_0','memb..., dimensions={0} | all-to-all | bytes 3149824 | tf_op jit(solution)/shard_map/all_to_all | solution.py:29
  115.6 0.0 copy-start.2
  115.6 0.3 convert_reduce_fusion
  115.9 0.1 slice_reduce_fusion
  116.0 0.0 copy-done.6
  116.0 0.4 fusion.14
  116.4 0.1 select_reduce_fusion.1
  116.5 0.4 reshape_reshape.7
  117.0 0.1 copy.42
  117.0 5.3 %all_to_all.59 = f32[2,64,385]{2,1,0:T(8,128)S(1)} all-to-all(f32[2,64,385]{2,1,0:T(8,128)S(1)} %copy.42), channel_id=1, replica_groups=mesh['group'=4,'member_0'=4,'member_1'=4,'member_2'=2] {'member_2'}, dimensions={0} | all-to-all | bytes 394240 | tf_op jit(solution)/shard_map/all_to_all | solution.py:70
  122.4 0.7 all_to_all.42
  123.1 4.8 %all-to-all-start.5 = ((f32[64,1,385]{2,1,0:T(1,128)}), f32[64,1,385]{2,1,0:T(1,128)S(1)}, u32[]{:S(2)}, u32[]{:S(2)}) async-start(f32[64,1,385]{2,1,0:T(1,128)} %all_to_all.42), calls=%async_computation.5 | async-start | bytes 262144 | tf_op jit(solution)/shard_map/all_to_all | solution.py:77
  127.9 0.0 copy-done.2
  128.0 0.6 convolution_convert_fusion
  128.5 2.0 %copy.44 = bf16[128,8,768]{2,1,0:T(8,128)(2,1)} copy(bf16[128,8,768]{2,0,1:T(8,128)(2,1)S(1)} %bitcast.49) | data formatting | bytes 3145728 | tf_op jit(solution)/shard_map/reshape | solution.py:154
  130.6 6.1 %all-to-all-done.5 = f32[64,1,385]{2,1,0:T(1,128)S(1)} async-done(((f32[64,1,385]{2,1,0:T(1,128)}), f32[64,1,385]{2,1,0:T(1,128)S(1)}, u32[]{:S(2)}, u32[]{:S(2)}) %all-to-all-start.5) | async-done | bytes 98592 | tf_op jit(solution)/shard_map/all_to_all | solution.py:77
  136.7 5.3 %all-to-all-start.8 = ((bf16[128,8,768]{2,1,0:T(8,128)(2,1)}), bf16[128,8,768]{2,1,0:T(8,128)(2,1)S(1)}, u32[]{:S(2)}, u32[]{:S(2)}) async-start(bf16[128,8,768]{2,1,0:T(8,128)(2,1)} %copy.44), calls=%async_computation.8 | async-start | bytes 3145728 | tf_op jit(solution)/shard_map/all_to_all | solution.py:155
  142.0 0.1 reduce_sum.112
  142.1 24.5 %all-to-all-done.8 = bf16[128,8,768]{2,1,0:T(8,128)(2,1)S(1)} async-done(((bf16[128,8,768]{2,1,0:T(8,128)(2,1)}), bf16[128,8,768]{2,1,0:T(8,128)(2,1)S(1)}, u32[]{:S(2)}, u32[]{:S(2)}) %all-to-all-start.8) | async-done | bytes 1572896 | tf_op jit(solution)/shard_map/all_to_all | solution.py:155
  166.6 0.7 broadcast_in_dim.21
  167.3 4.7 %all-to-all-start.6 = ((f32[64,1,385]{2,1,0:T(1,128)}), f32[64,1,385]{2,1,0:T(1,128)S(1)}, u32[]{:S(2)}, u32[]{:S(2)}) async-start(f32[64,1,385]{2,1,0:T(1,128)} %broadcast_in_dim.21), calls=%async_computation.6 | async-start | bytes 262144 | tf_op jit(solution)/shard_map/all_to_all | solution.py:53
  172.0 0.0 copy-start.3
  172.0 0.0 copy-start.4
  172.1 2.7 %gather_fusion = bf16[512,768]{1,0:T(8,128)(2,1)} fusion(bf16[1024,768]{1,0:T(8,128)(2,1)S(1)} %bitcast.45, s32[1024]{0:T(1024)S(1)} %pad_clamp_fusion), kind=kCustom, calls=%fused_computation | custom fusion | bytes 1574912 | tf_op jit(solution)/shard_map/gather | solution.py:156
  174.8 6.0 %all-to-all-done.6 = f32[64,1,385]{2,1,0:T(1,128)S(1)} async-done(((f32[64,1,385]{2,1,0:T(1,128)}), f32[64,1,385]{2,1,0:T(1,128)S(1)}, u32[]{:S(2)}, u32[]{:S(2)}) %all-to-all-start.6) | async-done | bytes 98592 | tf_op jit(solution)/shard_map/all_to_all | solution.py:53
  180.8 6.0 %all_to_all.60 = f32[2,64,385]{2,1,0:T(8,128)S(1)} all-to-all(f32[2,64,385]{2,1,0:T(8,128)S(1)} %broadcast_in_dim.22), channel_id=1, replica_groups=mesh['group'=4,'member_0'=4,'member_1'=4,'member_2'=2] {'member_2'}, dimensions={0} | all-to-all | bytes 394240 | tf_op jit(solution)/shard_map/all_to_all | solution.py:53
  186.9 0.2 copy.43
  187.1 0.3 reshape_reshape.8
  187.5 0.0 copy-done.3
  187.5 0.0 copy-done.4
  187.5 0.8 add_divide_fusion
  (16 shorter events, 0.2 us)
Async XLA Ops:
  2.2 20.9 %all-to-all-start = ((s32[128,1,4]{2,1,0:T(1,128)}), s32[128,1,4]{2,1,0:T(1,128)S(1)}, u32[]{:S(2)}, u32[]{:S(2)}) async-start(s32[128,1,4]{2,1,0:T(1,128)} %bitcast.1), calls=%async_computation | async-start | bytes 131072 | tf_op jit(solution)/shard_map/all_to_all | solution.py:131
  13.7 16.2 %copy-start = (bf16[1024,768]{1,0:T(8,128)(2,1)S(1)}, bf16[1024,768]{1,0:T(8,128)(2,1)}, u32[]{:S(2)}) copy-start(bf16[1024,768]{1,0:T(8,128)(2,1)} %param.10) | copy-start | bytes 4718596
  15.8 14.6 %copy-start.5 = (s32[1024]{0:T(1024)S(1)}, s32[1024]{0:T(1024)}, u32[]{:S(2)}) copy-start(s32[1024]{0:T(1024)} %param.12) | copy-start | bytes 12292
  23.1 31.4 %all-to-all-start.1 = ((bf16[128,8,768]{2,1,0:T(8,128)(2,1)}), bf16[128,8,768]{2,1,0:T(8,128)(2,1)S(1)}, u32[]{:S(2)}, u32[]{:S(2)}) async-start(bf16[128,8,768]{2,1,0:T(8,128)(2,1)} %bitcast.5), calls=%async_computation.1 | async-start | bytes 3145728 | tf_op jit(solution)/shard_map/all_to_all | solution.py:130
  29.9 26.0 %copy-start.7 = (f32[4]{0:T(128)S(1)}, f32[4]{0:T(128)}, u32[]{:S(2)}) copy-start(f32[4]{0:T(128)} %param.11) | copy-start | bytes 52
  58.5 5.5 %copy-start.1 = (bf16[128,4,2,256]{3,0,2,1:T(8,128)(2,1)}, bf16[128,4,2,256]{3,0,2,1:T(8,128)(2,1)S(1)}, u32[]{:S(2)}) copy-start(bf16[128,4,2,256]{3,0,2,1:T(8,128)(2,1)S(1)} %get-tuple-element.7) | copy-start | bytes 1572868
  88.4 27.6 %copy-start.6 = (s32[64]{0:T(128)S(1)}, s32[64]{0:T(128)}, u32[]{:S(2)}) copy-start(s32[64]{0:T(128)} %param.14) | copy-start | bytes 772
  115.6 12.3 %copy-start.2 = (bf16[128,4,2,256]{3,0,2,1:T(8,128)(2,1)S(1)}, bf16[128,4,2,256]{3,0,2,1:T(8,128)(2,1)}, u32[]{:S(2)}) copy-start(bf16[128,4,2,256]{3,0,2,1:T(8,128)(2,1)} %copy-done.1) | copy-start | bytes 1572868
  123.1 13.6 %all-to-all-start.5 = ((f32[64,1,385]{2,1,0:T(1,128)}), f32[64,1,385]{2,1,0:T(1,128)S(1)}, u32[]{:S(2)}, u32[]{:S(2)}) async-start(f32[64,1,385]{2,1,0:T(1,128)} %all_to_all.42), calls=%async_computation.5 | async-start | bytes 262144 | tf_op jit(solution)/shard_map/all_to_all | solution.py:77
  136.7 29.9 %all-to-all-start.8 = ((bf16[128,8,768]{2,1,0:T(8,128)(2,1)}), bf16[128,8,768]{2,1,0:T(8,128)(2,1)S(1)}, u32[]{:S(2)}, u32[]{:S(2)}) async-start(bf16[128,8,768]{2,1,0:T(8,128)(2,1)} %copy.44), calls=%async_computation.8 | async-start | bytes 3145728 | tf_op jit(solution)/shard_map/all_to_all | solution.py:155
  167.3 13.5 %all-to-all-start.6 = ((f32[64,1,385]{2,1,0:T(1,128)}), f32[64,1,385]{2,1,0:T(1,128)S(1)}, u32[]{:S(2)}, u32[]{:S(2)}) async-start(f32[64,1,385]{2,1,0:T(1,128)} %broadcast_in_dim.21), calls=%async_computation.6 | async-start | bytes 262144 | tf_op jit(solution)/shard_map/all_to_all | solution.py:53
  172.0 15.5 %copy-start.3 = (f32[64,768]{1,0:T(8,128)S(1)}, f32[64,768]{1,0:T(8,128)}, u32[]{:S(2)}) copy-start(f32[64,768]{1,0:T(8,128)} %param.15) | copy-start | bytes 589828
  172.0 15.5 %copy-start.4 = (f32[64,768]{1,0:T(8,128)S(1)}, f32[64,768]{1,0:T(8,128)}, u32[]{:S(2)}) copy-start(f32[64,768]{1,0:T(8,128)} %param.13) | copy-start | bytes 589828
where the time goes:
time: 189 us; the launch traced here: 188 us
  waiting for transfers between devices  63.6 us (34%)
  blocking collectives  47.2 us (25%)
  starting transfers between devices  33.1 us (18%)
  matrix products  20.6 us (11%)
  local copies, waits for them, and re-layouts  14.4 us (8%)
  other arithmetic  8.51 us (5%)
    all_to_all x1, blocking collectives, sum_in_two_steps(): lax.all_to_all(nearer.astype(jnp.bfloat16), far, split_axis=0, concat_axi...  27.2 us
    all_to_all x1, waiting for transfers between devices, shards(): lax.all_to_all(rebuilt, GROUP_MEMBER, split_axis=0, concat_axis=0, tiled=...  24.5 us
    all_to_all x1, waiting for transfers between devices, shards(): lax.all_to_all(outgoing, GROUP_MEMBER, split_axis=0, concat_axis=0, tiled...  24 us
    dot_general x1, matrix products, shards(): mid_part = jnp.dot(picker.T, weighted_flat, precision=lax.Precision.HIGHEST)  12.3 us
    all_to_all x1, starting transfers between devices, shards(): lax.all_to_all(sent_counts, GROUP_MEMBER, split_axis=0, concat_axis=0, ti...  11.5 us
    all_to_all x1, blocking collectives, sent_and_summed(): lax.all_to_all(pieces, axis, split_axis=0, concat_axis=0, tiled=True)  8.69 us
    all_to_all x1, starting transfers between devices, shards(): lax.all_to_all(outgoing, GROUP_MEMBER, split_axis=0, concat_axis=0, tiled...  6.81 us
    all_to_all x1, waiting for transfers between devices, sum_in_two_steps_2(): return jnp.sum(lax.all_to_all(own, far, 0, 0, tiled=True), axis=0)  6.14 us
  transfers between devices with their start and end apart: 5, of which 5 were waited for; matrix products, arithmetic and copies ran while one was open for 7% of the time, Pallas kernels for 0%

commit v1 on v0

v1 whole, which is shorter than its diff:
```python
import functools
import math

import jax
import jax.numpy as jnp
from jax import lax
from jax.experimental import pallas as pl
from jax.experimental.pallas import tpu as pltpu
from jax.sharding import Mesh
from jax.sharding import PartitionSpec as P

MEMBER = ("member_0", "member_1", "member_2")
GROUP_MEMBER = ("group", "member_0", "member_1", "member_2")
RINGS = ("group", "member_0", "member_1")
CORE = "member_2"
EMPTY = 64.0
MESH_ID = pl.DeviceIdType.MESH


def split_up(array, dim, devices):
    dims = array.shape
    pieces = array.reshape(*dims[:dim], devices, dims[dim] // devices, *dims[dim + 1 :])
    return jnp.moveaxis(pieces, dim, 0)


def sent_and_summed(array, axis, dim):
    pieces = split_up(array, dim, lax.axis_size(axis))
    arrived = lax.all_to_all(pieces, axis, split_axis=0, concat_axis=0, tiled=True)
    return arrived.astype(jnp.float32).sum(axis=0)


def sum_in_two_steps(array, axes, dim):
    far, near = axes
    pieces = split_up(array, dim, lax.axis_size(far))
    nearer = sent_and_summed(pieces, near, dim + 1)
    arrived = lax.all_to_all(
        nearer.astype(jnp.bfloat16), far, split_axis=0, concat_axis=0, tiled=True
    )
    return arrived.astype(jnp.float32).sum(axis=0)


def filled_up(lines, devices):
    spare = -len(lines) % devices
    return jnp.pad(lines, [(0, spare)] + [(0, 0)] * (lines.ndim - 1))


def copy_for_each(array, axis):
    copies = jnp.broadcast_to(array, (lax.axis_size(axis), *array.shape))
    return lax.all_to_all(copies, axis, split_axis=0, concat_axis=0, tiled=True)


def in_order(pieces, dim):
    pieces = jnp.moveaxis(pieces, 0, dim)
    dims = pieces.shape
    return pieces.reshape(*dims[:dim], dims[dim] * dims[dim + 1], *dims[dim + 2 :])


def gathered_by_axis(array, axes, dim):
    far, near = axes
    pieces = copy_for_each(copy_for_each(array, far), near)
    return in_order(pieces.swapaxes(0, 1).reshape(-1, *array.shape), dim)


def sum_at_owner(array, axis, dim):
    pieces = split_up(array, dim, lax.axis_size(axis))
    arrived = lax.all_to_all(pieces, axis, split_axis=0, concat_axis=0, tiled=True)
    return arrived.sum(axis=0)


def sum_in_two_steps_2(array, axes, dim):
    far, near = axes
    own = sum_at_owner(split_up(array, dim, lax.axis_size(far)), near, dim + 1)
    return jnp.sum(lax.all_to_all(own, far, 0, 0, tiled=True), axis=0)


def sum_by_parts(array, axes):
    padded = filled_up(array, lax.axis_size(axes[0]) * lax.axis_size(axes[1]))
    whole = gathered_by_axis(sum_in_two_steps_2(padded, axes, 0), axes, 0)
    return lax.slice_in_dim(whole, 0, len(array)).reshape(array.shape)


class Wires:
    def __init__(self, send_sem, recv_sem):
        self.send_sem, self.recv_sem = send_sem, recv_sem
        self.sent, self.arrivals, self.last = 0, 0, []

    def slots(self, number):
        self.arrivals += number
        return self.arrivals - number

    def copy(self, source, target, to, send_at, recv_at):
        return pltpu.make_async_remote_copy(
            src_ref=source,
            dst_ref=target,
            send_sem=self.send_sem.at[send_at],
            recv_sem=self.recv_sem.at[recv_at],
            device_id=to,
            device_id_type=MESH_ID,
        )

    def send(self, source, target, to, recv_at):
        copy = self.copy(source, target, to, self.sent, recv_at)
        self.sent += 1
        copy.start()
        self.last.append(copy)

    def arrived(self, like, to, recv_at):
        self.copy(like, like, to, 0, recv_at).wait_recv()

    def drain(self):
        for copy in self.last:
            copy.wait_send()


def greet(peers):
    barrier = pltpu.get_barrier_semaphore()
    for peer in peers:
        pl.semaphore_signal(barrier, inc=1, device_id=peer, device_id_type=MESH_ID)
    pl.semaphore_wait(barrier, len(peers))


def ring_places(axis):
    me = lax.axis_index(axis)
    return me, lax.rem(me + 1, 4), lax.rem(me + 3, 4), lax.rem(me + 2, 4)


def ring_peers(both_cores):
    core = lax.axis_index(CORE)
    peers = [{CORE: 1 - core}]
    for axis in RINGS:
        for to in ring_places(axis)[1:]:
            peers.append({axis: to})
            if both_cores:
                peers.append({axis: to, CORE: 1 - core})
    return peers


def exchange_kernel(subs, in_ref, out_ref, *scratch):
    stage_a, stage_b, send_sem, recv_sem = scratch
    wires = Wires(send_sem, recv_sem)
    core = lax.axis_index(CORE)
    other = 1 - core
    rings = [ring_places(axis) for axis in RINGS]
    greet(ring_peers(True))
    refs = (in_ref, stage_a, stage_b, out_ref)
    chunks = range(3 * subs)

    def spot(chunk, dim, index, core_at=slice(None)):
        at = [chunk, slice(None), slice(None), slice(None), core_at]
        at[dim + 1] = index
        return tuple(at)

    def start(phase, chunk):
        dim = (chunk + phase) % 3
        source, target = refs[phase], refs[phase + 1]
        axis = RINGS[dim]
        me, up, down, across = rings[dim]
        if phase < 2:
            base = wires.slots(3)
            for way, to in enumerate((across, up, down)):
                wires.send(
                    source.at[spot(chunk, dim, to)],
                    target.at[spot(chunk, dim, me)],
                    {axis: to},
                    base + way,
                )
            own = spot(chunk, dim, me)
        else:
            base = wires.slots(7)
            for way, to in enumerate((across, up, down)):
                for core_at in (0, 1):
                    wires.send(
                        source.at[spot(chunk, dim, to, core_at)],
                        target.at[spot(chunk, dim, me, core)],
                        {axis: to, CORE: core_at},
                        base + 2 * way + core,
                    )
            wires.send(
                source.at[spot(chunk, dim, me, other)],
                target.at[spot(chunk, dim, me, core)],
                {CORE: other},
                base + 6,
            )
            own = spot(chunk, dim, me, core)
        target[own] = source[own]
        return base

    def finish(phase, chunk, base):
        dim = (chunk + phase) % 3
        me, up, _, _ = rings[dim]
        if phase < 2:
            like, number = refs[phase + 1].at[spot(chunk, dim, me)], 3
        else:
            like, number = refs[phase + 1].at[spot(chunk, dim, me, core)], 7
        for at in range(number):
            wires.arrived(like, {RINGS[dim]: up}, base + at)

    running = [start(0, chunk) for chunk in chunks]
    for phase in range(3):
        following = []
        for chunk in chunks:
            finish(phase, chunk, running[chunk])
            if phase < 2:
                following.append(start(phase + 1, chunk))
        running = following
    wires.drain()


def exchanged(array, collective_id):
    chunks, rows, lanes = array.shape
    shape = (chunks, 4, 4, 4, 2, rows // 128, lanes)
    copies = 13 * chunks
    moved = pl.pallas_call(
        functools.partial(exchange_kernel, chunks // 3),
        out_shape=jax.ShapeDtypeStruct(shape, array.dtype),
        in_specs=[pl.BlockSpec(memory_space=pltpu.VMEM)],
        out_specs=pl.BlockSpec(memory_space=pltpu.VMEM),
        scratch_shapes=[
            pltpu.VMEM(shape, array.dtype),
            pltpu.VMEM(shape, array.dtype),
            pltpu.SemaphoreType.DMA((copies,)),
            pltpu.SemaphoreType.DMA((copies,)),
        ],
        compiler_params=pltpu.CompilerParams(
            collective_id=collective_id, has_side_effects=True
        ),
        name=f"exchange_{collective_id}",
    )(array.reshape(shape))
    return moved.reshape(chunks, rows, lanes)


def shards(
    samples,
    cell_of_row,
    fine_centroids,
    sharpness,
    mid_of_fine,
    mid_centroids,
    coarse_of_mid,
    coarse_centroids,
):
    groups = lax.axis_size("group")
    members = lax.axis_size(MEMBER)
    devices = groups * members
    row_count = samples.shape[0]
    feature_width = samples.shape[1]
    cell_dev = sharpness.shape[0]
    fine_count = fine_centroids.shape[0] // cell_dev
    most_rows = 2 * row_count // (cell_dev * devices)
    total_cells = cell_dev * devices
    slots = total_cells * most_rows
    cell_ids = cell_of_row[:, 0]
    place = jnp.arange(row_count, dtype=jnp.int32)
    same = (cell_ids[:, None] == cell_ids[None, :]) & (place[:, None] < place[None, :])
    rank_in_cell = jnp.sum(same.astype(jnp.int32), axis=0)
    slot_index = cell_ids * most_rows + rank_in_cell
    picked = slot_index[None, :] == jnp.arange(slots, dtype=jnp.int32)[:, None]
    used = jnp.any(picked, axis=1)
    picked_rows = picked.astype(jnp.bfloat16)
    lanes = 128
    chunks = feature_width // lanes
    outgoing = jnp.einsum(
        "sr,rcw->csw",
        picked_rows,
        samples.reshape(row_count, chunks, lanes),
        preferred_element_type=jnp.float32,
    )
    outgoing = jnp.where(used[None, :, None], outgoing, EMPTY).astype(jnp.bfloat16)
    arrived = exchanged(outgoing, 0)
    arrived = (
        arrived.reshape(chunks, devices, cell_dev, most_rows, lanes)
        .transpose(2, 1, 3, 0, 4)
        .reshape(cell_dev, devices * most_rows, feature_width)
    )
    fine_local = fine_centroids.reshape(cell_dev, fine_count, feature_width)
    is_valid = arrived[..., 0].astype(jnp.float32) < 0.5 * EMPTY
    products = jnp.einsum("lrd,lkd->lrk", arrived, fine_local, preferred_element_type=jnp.float32)
    fine_float = fine_local.astype(jnp.float32)
    norms = jnp.sum(jnp.square(fine_float), axis=2)
    scores = (
        sharpness[:, None, None] * (products - 0.5 * norms[:, None, :]) / math.sqrt(feature_width)
    )
    highest = jnp.max(scores, axis=2, keepdims=True)
    exponent = jnp.exp(scores - highest)
    probs = exponent / jnp.sum(exponent, axis=2, keepdims=True)
    resp = jnp.where(is_valid[..., None], probs, 0.0).astype(jnp.bfloat16)
    weighted = jnp.einsum("lrk,lrd->lkd", resp, arrived, preferred_element_type=jnp.float32)
    mass_total = jnp.sum(resp.astype(jnp.float32), axis=1)
    fine_new = (weighted + fine_float) / (mass_total[..., None] + 1.0)
    rebuilt = jnp.einsum(
        "lrk,lkd->lrd", resp, fine_local, preferred_element_type=jnp.float32
    ).astype(jnp.bfloat16)
    rebuilt = (
        rebuilt.reshape(cell_dev, devices, most_rows, chunks, lanes)
        .transpose(3, 1, 0, 2, 4)
        .reshape(chunks, slots, lanes)
    )
    returned = exchanged(rebuilt, 1)
    reconstruction = jnp.einsum(
        "sr,csw->rcw", picked_rows, returned, preferred_element_type=jnp.float32
    )
    reconstruction = reconstruction.astype(jnp.bfloat16).reshape(row_count, feature_width)
    group_index = lax.axis_index("group")
    mid_dev = mid_centroids.shape[0]
    mid_group = mid_dev * members
    local_mid = mid_of_fine - group_index * mid_group
    picker = (local_mid[:, None] == jnp.arange(mid_group, dtype=jnp.int32)[None, :]).astype(
        jnp.bfloat16
    )
    weighted_flat = weighted.reshape(cell_dev * fine_count, feature_width)
    mass_flat = mass_total.reshape(cell_dev * fine_count)
    both = jnp.concatenate(
        [
            weighted_flat.astype(jnp.bfloat16),
            jnp.broadcast_to(mass_flat[:, None], (len(mass_flat), 128)).astype(jnp.bfloat16),
        ],
        axis=1,
    )
    mid_part = jnp.dot(picker.T, both, preferred_element_type=jnp.float32)[:, : feature_width + 1]
    own = sum_in_two_steps(mid_part.astype(jnp.bfloat16), (("member_0", "member_1"), "member_2"), 0)
    own_sum, own_count = own[:, :feature_width], own[:, feature_width]
    mids_new = (own_sum + mid_centroids) / (own_count[:, None] + 1.0)
    coarse_total = coarse_centroids.shape[0]
    coarse_route = (
        coarse_of_mid[:, None] == jnp.arange(coarse_total, dtype=jnp.int32)[None, :]
    ).astype(jnp.float32)
    coarse_part = jnp.dot(coarse_route.T, own, precision=lax.Precision.HIGHEST)
    coarse_all = sum_by_parts(coarse_part, (("group", "member_0", "member_1"), "member_2"))
    coarse_sums, coarse_counts = coarse_all[:, :feature_width], coarse_all[:, feature_width]
    coarse_new = (coarse_sums + coarse_centroids) / (coarse_counts[:, None] + 1.0)
    return (
        fine_new.reshape(cell_dev * fine_count, feature_width),
        mids_new,
        coarse_new,
        reconstruction,
    )


def solution(mesh):
    split = Mesh(
        mesh.devices.reshape(mesh.shape["group"], 4, 4, 2),
        ("group", "member_0", "member_1", "member_2"),
    )
    placed = (
        P(GROUP_MEMBER, None),
        P(GROUP_MEMBER, None),
        P(GROUP_MEMBER, None),
        P(GROUP_MEMBER),
        P(GROUP_MEMBER),
        P(GROUP_MEMBER, None),
        P(GROUP_MEMBER),
        P(),
    )
    return jax.shard_map(
        shards,
        mesh=split,
        in_specs=placed,
        out_specs=(P(GROUP_MEMBER, None), P(GROUP_MEMBER, None), P(), P(GROUP_MEMBER, None)),
        check_vma=False,
    )
```

time: 189 us -> 184 us (0.974)
  Pallas kernels: 0 us -> 60.9 us
  waiting for transfers between devices: 63.6 us -> 6.92 us
  starting transfers between devices: 33.1 us -> 11.3 us
  local copies, waits for them, and re-layouts: 14.4 us -> 25.8 us
  other arithmetic: 8.51 us -> 11.7 us
  matrix products: 20.6 us -> 18.7 us
    pallas_call x0 -> x2, Pallas kernels: none -> 60.9 us  [exchanged(): pl.pallas_call(functools.partial(exchange_kernel, chunks // 3), out_shape...]
    all_to_all x3 -> x0, waiting for transfers between devices: 51.4 us -> none  [the longest x1 24.5 us: shards(): lax.all_to_all(rebuilt, GROUP_MEMBER, split_axis=0, concat_axis=0, tiled=...]
    all_to_all x3 -> x0, starting transfers between devices: 23.6 us -> none  [the longest x1 11.5 us: shards(): lax.all_to_all(sent_counts, GROUP_MEMBER, split_axis=0, concat_axis=0, ti...]
    all_to_all x1, waiting for transfers between devices: 6.14 us -> 0.01 us  [sum_in_two_steps_2(): return jnp.sum(lax.all_to_all(own, far, 0, 0, tiled=True), axis=0)]
    reshape x3, local copies, waits for them, and re-layouts: 2.07 us -> 7.8 us  [the longest x1 3.38 us: shards(): rebuilt.reshape(cell_dev, devices, most_rows, chunks, lanes)]
    slice x1 -> x5, local copies, waits for them, and re-layouts: 0.01 us -> 4.76 us  [the longest x2 4.41 us: shards(): jnp.dot(picker.T, both, preferred_element_type=jnp.float32)]
    scatter x1 -> x0, local copies, waits for them, and re-layouts: 4.37 us -> none  [shards(): outgoing = jnp.zeros((total_cells * most_rows, feature_width), jnp.bfloat...]
    dot_general x5, matrix products: 18.3 us -> 14.4 us  [the longest x1 6.23 us: shards(): jnp.dot(picker.T, both, preferred_element_type=jnp.float32)]
  transfers between devices with their start and end apart: 5 -> 2, of which waited for: 5 -> 1; matrix products, arithmetic and copies ran while one was open for 7% -> 6% of each run, Pallas kernels for 0% -> 16%
where the time goes in v1:
time: 184 us; the launch traced here: 183 us
  Pallas kernels  60.9 us (33%)
  blocking collectives  46.9 us (25%)
  local copies, waits for them, and re-layouts  25.8 us (14%)
  matrix products  18.7 us (10%)
  other arithmetic  11.7 us (6%)
  starting transfers between devices  11.3 us (6%)
  waiting for transfers between devices  6.92 us (4%)
    pallas_call x2, Pallas kernels, exchanged(): pl.pallas_call(functools.partial(exchange_kernel, chunks // 3), out_shape...  60.9 us
    all_to_all x1, blocking collectives, sum_in_two_steps(): lax.all_to_all(nearer.astype(jnp.bfloat16), far, split_axis=0, concat_axi...  28 us
    all_to_all x1, blocking collectives, sent_and_summed(): lax.all_to_all(pieces, axis, split_axis=0, concat_axis=0, tiled=True)  7.73 us
    all_to_all x1, waiting for transfers between devices, copy_for_each(): return lax.all_to_all(copies, axis, split_axis=0, concat_axis=0, tiled=True)  6.92 us
    dot_general x1, matrix products, shards(): jnp.dot(picker.T, both, preferred_element_type=jnp.float32)  6.23 us
    all_to_all x1, starting transfers between devices, copy_for_each(): return lax.all_to_all(copies, axis, split_axis=0, concat_axis=0, tiled=True)  6.03 us
    all_to_all x1, blocking collectives, sum_at_owner(): lax.all_to_all(pieces, axis, split_axis=0, concat_axis=0, tiled=True)  5.59 us
    all_to_all x1, blocking collectives, copy_for_each(): return lax.all_to_all(copies, axis, split_axis=0, concat_axis=0, tiled=True)  5.57 us
  transfers between devices with their start and end apart: 2, of which 1 were waited for; matrix products, arithmetic and copies ran while one was open for 6% of the time, Pallas kernels for 16%

profile of v1, /device:TPU:1, one launch (start us, length us, event | category | flops | bytes accessed | tf_op | source)
XLA Modules:
  0.0 183.2 jit_solution(4183315464930419593)
XLA Ops:
  0.6 1.4 copy.47
  2.0 0.9 convert_reduce_fusion.2
  3.0 0.7 multiply_add_fusion
  3.7 0.3 fusion.5
  4.0 2.2 %select_convert_fusion = bf16[1024,6,128]{2,0,1:T(8,128)(2,1)} fusion(bf16[512,6,128]{0,2,1:T(8,128)(2,1)S(1)} %bitcast.63, pred[1024]{0:T(1024)(128)(4,1)S(1)} %fusion.5, s32[512]{0:T(512)S(1)} %multiply_add_fusion), kind=kOutput, calls=%fused_computation.8 | convolution fusion | flops 807403520 | bytes 2362368 | tf_op jit(solution)/shard_map/sr,rcw->csw/dot_general | solution.py:262
  6.2 31.6 %exchange_0.1 = bf16[6,4,4,4,2,8,128]{6,5,4,3,2,1,0:T(8,128)(2,1)} custom-call(bf16[6,4,4,4,2,8,128]{6,5,4,3,2,1,0:T(8,128)(2,1)} %bitcast.59), custom_call_target="tpu_custom_call" | custom-call | tf_op jit(solution)/shard_map/exchange_0/pallas_call | solution.py:213
  37.8 3.3 %copy.64 = bf16[6,128,4,2,128]{4,0,3,1,2:T(8,128)(2,1)S(1)} copy(bf16[6,128,4,2,128]{4,3,2,1,0:T(2,128)(2,1)} %bitcast.53) | data formatting | bytes 3145728 | tf_op jit(solution)/shard_map/reshape;reshape | solution.py:271
  41.1 2.7 %reshape.73 = bf16[4,256,768]{2,1,0:T(8,128)(2,1)} reshape(bf16[4,128,2,6,128]{4,3,2,1,0:T(8,128)(2,1)S(1)} %bitcast.48) | data formatting | bytes 3145728 | tf_op jit(solution)/shard_map/reshape | solution.py:273
  43.8 0.0 copy-start
  43.8 0.0 copy-start.8
  43.8 1.9 %multiply_reduce_fusion = f32[1024]{0:T(1024)S(1)} fusion(bf16[1024,768]{1,0:T(8,128)(2,1)} %param.10), kind=kLoop, calls=%fused_computation.7 | loop fusion | flops 2358272 | bytes 1576960 | tf_op jit(solution)/shard_map/reduce_sum | solution.py:279
  45.8 1.2 fusion.20
  46.9 0.0 copy-done
  46.9 0.0 copy-done.8
  47.0 0.0 copy-start.2
  47.0 3.3 %fusion.29 = (f32[4,256]{1,0:T(4,128)S(1)}, f32[4,256,256]{1,2,0:T(8,128)}) fusion(bf16[4,256,768]{2,1,0:T(8,128)(2,1)} %reshape.73, bf16[4,256,768]{2,1,0:T(8,128)(2,1)S(1)} %bitcast.50, f32[4,256]{1,0:T(4,128)S(1)} %mul.40, f32[4]{0:T(128)S(1)} %copy-done.8), kind=kOutput, calls=%fused_computation.52 | convolution fusion | flops 403964160 | bytes 4202512 | tf_op jit(solution)/shard_map/sub | solution.py:284
  50.2 2.1 %convert_reduce_fusion.1 = (f32[4,256]{1,0:T(4,128)S(1)}, bf16[4,256,256]{1,2,0:T(8,128)(2,1)}) fusion(f32[4,256,256]{1,2,0:T(8,128)} %get-tuple-element.31, f32[4,256]{1,0:T(4,128)S(1)} %get-tuple-element.30, pred[4,256]{1,0:T(4,128)(4,1)S(1)} %fusion.20), kind=kLoop, calls=%fused_computation.24 | loop fusion | flops 1309696 | bytes 1582080 | tf_op jit(solution)/shard_map/reduce_sum | solution.py:288
  52.4 0.0 copy-done.2
  52.4 0.0 copy-start.6
  52.4 3.8 %fusion.28 = (bf16[4,256,768]{2,1,0:T(8,128)(2,1)}, f32[4,256,768]{2,1,0:T(8,128)}) fusion(f32[4,256]{1,0:T(4,128)S(1)} %get-tuple-element.29, bf16[4,256,768]{2,1,0:T(8,128)(2,1)S(1)} %bitcast.51, bf16[4,256,256]{1,2,0:T(8,128)(2,1)} %get-tuple-element.25, bf16[4,256,768]{2,1,0:T(8,128)(2,1)S(1)} %copy-done.2), kind=kOutput, calls=%fused_computation.51 | convolution fusion | flops 405798912 | bytes 8392704 | tf_op jit(solution)/shard_map/lrk,lrd->lkd/dot_general | solution.py:287
  56.2 0.0 copy-done.6
  56.2 0.2 broadcast_in_dim.57
  56.4 6.2 %fusion.1 = bf16[2048,896]{0,1:T(8,128)(2,1)S(1)} fusion(s32[1024]{0:T(1024)S(1)} %broadcast_subtract_fusion, bf16[1024,128]{1,0:T(8,128)(2,1)S(1)} %broadcast_in_dim.57, bf16[1024,768]{1,0:T(8,128)(2,1)} %bitcast.68), kind=kOutput, calls=%fused_computation.2 | convolution fusion | flops 3763863552 | bytes 5509120 | tf_op jit(solution)/shard_map/dot_general | solution.py:319
  62.7 0.4 slice.54
  63.1 4.0 %copy.50 = bf16[2048,769]{1,0:T(8,128)(2,1)} copy(bf16[2048,769]{0,1:T(8,128)(2,1)S(1)} %slice.54) | data formatting | bytes 6299648 | tf_op jit(solution)/shard_map/slice | solution.py:319
  67.1 2.4 %copy.51 = bf16[2,16,64,769]{3,2,1,0:T(8,128)(2,1)S(1)} copy(bf16[2,16,64,769]{3,2,0,1:T(8,128)(2,1)} %bitcast.47) | data formatting | bytes 6299648 | tf_op jit(solution)/shard_map/transpose | solution.py:23
  69.5 7.7 %all_to_all.33 = bf16[2,16,64,769]{3,2,1,0:T(8,128)(2,1)} all-to-all(bf16[2,16,64,769]{3,2,1,0:T(8,128)(2,1)S(1)} %copy.51), channel_id=1, replica_groups=mesh['group'=4,'member_0'=4,'member_1'=4,'member_2'=2] {'member_2'}, dimensions={0} | all-to-all | bytes 6299648 | tf_op jit(solution)/shard_map/all_to_all | solution.py:28
  77.2 3.0 %reduce_sum.81 = bf16[16,64,769]{2,1,0:T(8,128)(2,1)S(1)} reduce(bf16[2,16,64,769]{3,2,1,0:T(8,128)(2,1)} %all_to_all.33, bf16[]{:T(256)} %constant.32.clone.1), dimensions={0}, to_apply=%region_6.7 | reduce | flops 787456 | bytes 4724738 | tf_op jit(solution)/shard_map/reduce_sum | solution.py:29
  80.2 28.0 %all_to_all.34 = bf16[16,64,769]{2,1,0:T(8,128)(2,1)S(1)} all-to-all(bf16[16,64,769]{2,1,0:T(8,128)(2,1)S(1)} %reduce_sum.81), channel_id=1, replica_groups=mesh['group'=4,'member_0'=4,'member_1'=4,'member_2'=2] {'member_0','memb..., dimensions={0} | all-to-all | bytes 3149824 | tf_op jit(solution)/shard_map/all_to_all | solution.py:36
  108.2 0.0 copy-start.7
  108.2 0.3 convert_reduce_fusion
  108.5 0.4 copy-done.7
  108.8 0.4 fusion.25
  109.3 0.3 reshape_reshape.15
  109.5 0.0 copy-start.1
  109.5 0.0 copy-start.3
  109.6 5.6 %all_to_all.35 = f32[2,64,1,769]{3,1,2,0:T(8,128)S(1)} all-to-all(f32[2,64,1,769]{3,1,2,0:T(8,128)S(1)} %copy.52), channel_id=1, replica_groups=mesh['group'=4,'member_0'=4,'member_1'=4,'member_2'=2] {'member_2'}, dimensions={0} | all-to-all | bytes 787456 | tf_op jit(solution)/shard_map/all_to_all | solution.py:66
  115.2 0.9 reduce_sum.84
  116.1 5.3 %all-to-all-start.3 = ((f32[64,1,769]{2,1,0:T(1,128)}), f32[64,1,769]{2,1,0:T(1,128)S(1)}, u32[]{:S(2)}, u32[]{:S(2)}) async-start(f32[64,1,769]{2,1,0:T(1,128)} %reduce_sum.84), calls=%async_computation.3 | async-start | bytes 458752 | tf_op jit(solution)/shard_map/all_to_all | solution.py:73
  121.4 0.0 copy-done.1
  121.4 0.0 copy-done.3
  121.4 1.8 convolution_convert_fusion
  123.2 3.4 %reshape.76 = bf16[4,128,2,6,128]{4,3,2,1,0:T(8,128)(2,1)S(1)} reshape(bf16[4,256,768]{2,1,0:T(8,128)(2,1)} %convolution_convert_fusion) | data formatting | bytes 3145728 | tf_op jit(solution)/shard_map/reshape | solution.py:294
  126.6 2.4 %copy.55 = bf16[6,128,4,2,128]{4,3,2,1,0:T(2,128)(2,1)} copy(bf16[6,128,4,2,128]{4,0,3,1,2:T(8,128)(2,1)S(1)} %bitcast.49) | data formatting | bytes 3145728 | tf_op jit(solution)/shard_map/transpose | solution.py:295
  128.9 29.3 %exchange_1.1 = bf16[6,4,4,4,2,8,128]{6,5,4,3,2,1,0:T(8,128)(2,1)} custom-call(bf16[6,4,4,4,2,8,128]{6,5,4,3,2,1,0:T(8,128)(2,1)} %bitcast.54), custom_call_target="tpu_custom_call" | custom-call | tf_op jit(solution)/shard_map/exchange_1/pallas_call | solution.py:213
  158.2 1.7 copy.56
  159.9 0.0 all-to-all-done.3
  159.9 0.2 reduce_sum.85
  160.1 0.8 broadcast_in_dim.58
  160.9 6.0 %all-to-all-start.4 = ((f32[64,1,769]{2,1,0:T(1,128)}), f32[64,1,769]{2,1,0:T(1,128)S(1)}, u32[]{:S(2)}, u32[]{:S(2)}) async-start(f32[64,1,769]{2,1,0:T(1,128)} %broadcast_in_dim.58), calls=%async_computation.4 | async-start | bytes 458752 | tf_op jit(solution)/shard_map/all_to_all | solution.py:49
  166.9 1.0 fusion.3
  168.0 0.1 convert_element_type.69
  168.1 1.2 copy.57
  169.2 0.0 copy-start.4
  169.2 0.0 copy-start.5
  169.2 0.1 fusion.24
  169.3 6.9 %all-to-all-done.4 = f32[64,1,769]{2,1,0:T(1,128)S(1)} async-done(((f32[64,1,769]{2,1,0:T(1,128)}), f32[64,1,769]{2,1,0:T(1,128)S(1)}, u32[]{:S(2)}, u32[]{:S(2)}) %all-to-all-start.4) | async-done | bytes 196896 | tf_op jit(solution)/shard_map/all_to_all | solution.py:49
  176.3 5.6 %all_to_all.36 = f32[2,64,1,769]{3,1,2,0:T(8,128)S(1)} all-to-all(f32[2,64,1,769]{3,1,2,0:T(8,128)S(1)} %broadcast_in_dim.59), channel_id=1, replica_groups=mesh['group'=4,'member_0'=4,'member_1'=4,'member_2'=2] {'member_2'}, dimensions={0} | all-to-all | bytes 787456 | tf_op jit(solution)/shard_map/all_to_all | solution.py:49
  181.9 0.2 copy.53
  182.1 0.2 slice.30
  182.3 0.1 fusion.23
  182.4 0.0 copy-done.4
  182.4 0.0 copy-done.5
  182.4 0.8 fusion.21
  (11 shorter events, 0.2 us)
Async XLA Ops:
  43.8 3.1 %copy-start = (bf16[1024,768]{1,0:T(8,128)(2,1)S(1)}, bf16[1024,768]{1,0:T(8,128)(2,1)}, u32[]{:S(2)}) copy-start(bf16[1024,768]{1,0:T(8,128)(2,1)} %param.10) | copy-start | bytes 4718596
  43.8 3.1 %copy-start.8 = (f32[4]{0:T(128)S(1)}, f32[4]{0:T(128)}, u32[]{:S(2)}) copy-start(f32[4]{0:T(128)} %param.11) | copy-start | bytes 52
  47.0 5.4 %copy-start.2 = (bf16[4,256,768]{2,1,0:T(8,128)(2,1)S(1)}, bf16[4,256,768]{2,1,0:T(8,128)(2,1)}, u32[]{:S(2)}) copy-start(bf16[4,256,768]{2,1,0:T(8,128)(2,1)} %reshape.73) | copy-start | bytes 4718596
  52.4 3.8 %copy-start.6 = (s32[1024]{0:T(1024)S(1)}, s32[1024]{0:T(1024)}, u32[]{:S(2)}) copy-start(s32[1024]{0:T(1024)} %param.12) | copy-start | bytes 12292
  108.2 0.7 copy-start.7
  109.5 11.8 %copy-start.1 = (bf16[1024,768]{1,0:T(8,128)(2,1)S(1)}, bf16[1024,768]{1,0:T(8,128)(2,1)}, u32[]{:S(2)}) copy-start(bf16[1024,768]{1,0:T(8,128)(2,1)} %param.10) | copy-start | bytes 4718596
  109.5 11.8 %copy-start.3 = (bf16[4,256,256]{1,2,0:T(8,128)(2,1)S(1)}, bf16[4,256,256]{1,2,0:T(8,128)(2,1)}, u32[]{:S(2)}) copy-start(bf16[4,256,256]{1,2,0:T(8,128)(2,1)} %get-tuple-element.25) | copy-start | bytes 1572868
  116.1 43.8 %all-to-all-start.3 = ((f32[64,1,769]{2,1,0:T(1,128)}), f32[64,1,769]{2,1,0:T(1,128)S(1)}, u32[]{:S(2)}, u32[]{:S(2)}) async-start(f32[64,1,769]{2,1,0:T(1,128)} %reduce_sum.84), calls=%async_computation.3 | async-start | bytes 458752 | tf_op jit(solution)/shard_map/all_to_all | solution.py:73
  160.9 15.4 %all-to-all-start.4 = ((f32[64,1,769]{2,1,0:T(1,128)}), f32[64,1,769]{2,1,0:T(1,128)S(1)}, u32[]{:S(2)}, u32[]{:S(2)}) async-start(f32[64,1,769]{2,1,0:T(1,128)} %broadcast_in_dim.58), calls=%async_computation.4 | async-start | bytes 458752 | tf_op jit(solution)/shard_map/all_to_all | solution.py:49
  169.2 13.1 %copy-start.4 = (f32[64,768]{1,0:T(8,128)S(1)}, f32[64,768]{1,0:T(8,128)}, u32[]{:S(2)}) copy-start(f32[64,768]{1,0:T(8,128)} %param.15) | copy-start | bytes 589828
  169.2 13.1 %copy-start.5 = (f32[64,768]{1,0:T(8,128)S(1)}, f32[64,768]{1,0:T(8,128)}, u32[]{:S(2)}) copy-start(f32[64,768]{1,0:T(8,128)} %param.13) | copy-start | bytes 589828

commit v2 on v1

v2 whole, which is shorter than its diff:
```python
import functools
import math

import jax
import jax.numpy as jnp
from jax import lax
from jax.experimental import pallas as pl
from jax.experimental.pallas import tpu as pltpu
from jax.sharding import Mesh
from jax.sharding import PartitionSpec as P

MEMBER = ("member_0", "member_1", "member_2")
GROUP_MEMBER = ("group", "member_0", "member_1", "member_2")
RINGS = ("group", "member_0", "member_1")
CORE = "member_2"
EMPTY = 64.0
MESH_ID = pl.DeviceIdType.MESH


class Wires:
    def __init__(self, send_sem, recv_sem):
        self.send_sem, self.recv_sem = send_sem, recv_sem
        self.sent, self.arrivals, self.last = 0, 0, []

    def slots(self, number):
        self.arrivals += number
        return self.arrivals - number

    def copy(self, source, target, to, send_at, recv_at):
        return pltpu.make_async_remote_copy(
            src_ref=source,
            dst_ref=target,
            send_sem=self.send_sem.at[send_at],
            recv_sem=self.recv_sem.at[recv_at],
            device_id=to,
            device_id_type=MESH_ID,
        )

    def send(self, source, target, to, recv_at):
        copy = self.copy(source, target, to, self.sent, recv_at)
        self.sent += 1
        copy.start()
        self.last.append(copy)

    def arrived(self, like, to, recv_at):
        self.copy(like, like, to, 0, recv_at).wait_recv()

    def drain(self):
        for copy in self.last:
            copy.wait_send()


def greet(peers):
    barrier = pltpu.get_barrier_semaphore()
    for peer in peers:
        pl.semaphore_signal(barrier, inc=1, device_id=peer, device_id_type=MESH_ID)
    pl.semaphore_wait(barrier, len(peers))


def ring_places(axis):
    me = lax.axis_index(axis)
    return me, lax.rem(me + 1, 4), lax.rem(me + 3, 4), lax.rem(me + 2, 4)


def ring_peers(both_cores):
    core = lax.axis_index(CORE)
    peers = [{CORE: 1 - core}]
    for axis in RINGS:
        for to in ring_places(axis)[1:]:
            peers.append({axis: to})
            if both_cores:
                peers.append({axis: to, CORE: 1 - core})
    return peers


class Exchange:
    def __init__(self, wires, refs):
        self.wires, self.refs = wires, refs
        self.core = lax.axis_index(CORE)
        self.rings = [ring_places(axis) for axis in RINGS]
        self.chunks = range(refs[0].shape[0])
        self.running = [None] * len(self.chunks)

    def spot(self, chunk, dim, index, core_at=slice(None)):
        at = [chunk, slice(None), slice(None), slice(None), core_at]
        at[dim + 1] = index
        return tuple(at)

    def start(self, phase, chunk):
        wires, core, other = self.wires, self.core, 1 - self.core
        dim = (chunk + phase) % 3
        source, target = self.refs[phase], self.refs[phase + 1]
        axis = RINGS[dim]
        me, up, down, across = self.rings[dim]
        if phase < 2:
            base = wires.slots(3)
            for way, to in enumerate((across, up, down)):
                wires.send(
                    source.at[self.spot(chunk, dim, to)],
                    target.at[self.spot(chunk, dim, me)],
                    {axis: to},
                    base + way,
                )
            own = self.spot(chunk, dim, me)
        else:
            base = wires.slots(7)
            for way, to in enumerate((across, up, down)):
                for core_at in (0, 1):
                    wires.send(
                        source.at[self.spot(chunk, dim, to, core_at)],
                        target.at[self.spot(chunk, dim, me, core)],
                        {axis: to, CORE: core_at},
                        base + 2 * way + core,
                    )
            wires.send(
                source.at[self.spot(chunk, dim, me, other)],
                target.at[self.spot(chunk, dim, me, core)],
                {CORE: other},
                base + 6,
            )
            own = self.spot(chunk, dim, me, core)
        target[own] = source[own]
        self.running[chunk] = base

    def finish(self, phase, chunk):
        dim = (chunk + phase) % 3
        me, up, _, _ = self.rings[dim]
        if phase < 2:
            like, number = self.refs[phase + 1].at[self.spot(chunk, dim, me)], 3
        else:
            like, number = self.refs[phase + 1].at[self.spot(chunk, dim, me, self.core)], 7
        for at in range(number):
            self.wires.arrived(like, {RINGS[dim]: up}, self.running[chunk] + at)

    def begin(self):
        for chunk in self.chunks:
            self.start(0, chunk)

    def advance(self, phase):
        for chunk in self.chunks:
            self.finish(phase, chunk)
            if phase < 2:
                self.start(phase + 1, chunk)


class Octet:
    def __init__(self, wires):
        self.wires = wires
        self.me = lax.axis_index("member_0") * 2 + lax.axis_index(CORE)

    def start(self, source_of, target):
        self.base = self.wires.slots(7)
        for step in range(1, 8):
            to = lax.rem(self.me + step, 8)
            where = {"member_0": to // 2, CORE: lax.rem(to, 2)}
            self.wires.send(source_of(to), target, where, self.base + step - 1)

    def finish(self, like):
        for step in range(7):
            self.wires.arrived(like, {CORE: 1 - lax.axis_index(CORE)}, self.base + step)


class Ring:
    def __init__(self, wires, axis):
        self.wires, self.axis = wires, axis
        self.me, self.up, self.down, self.across = ring_places(axis)

    def order(self):
        return (self.across, self.up, self.down)

    def open(self):
        self.base = self.wires.slots(3)

    def send(self, way, source, target):
        self.wires.send(source, target, {self.axis: self.order()[way]}, self.base + way)

    def start(self, source_of, target):
        self.open()
        for way, to in enumerate(self.order()):
            self.send(way, source_of(to), target)

    def finish(self, like):
        for way in range(3):
            self.wires.arrived(like, {self.axis: self.up}, self.base + way)


def rows_kernel(in_ref, map_ref, out_ref, maps_ref, stage_a, stage_b, send_sem, recv_sem):
    wires = Wires(send_sem, recv_sem)
    greet(ring_peers(True))
    moving = Exchange(wires, (in_ref, stage_a, stage_b, out_ref))
    moving.begin()
    octet, ring = Octet(wires), Ring(wires, "member_1")
    mine = maps_ref.at[ring.me, octet.me]
    octet.start(lambda to: map_ref, mine)
    maps_ref[ring.me, octet.me] = map_ref[...]
    octet.finish(mine)
    ring.start(lambda to: maps_ref.at[ring.me], maps_ref.at[ring.me])
    moving.advance(0)
    ring.finish(maps_ref.at[ring.me])
    moving.advance(1)
    moving.advance(2)
    wires.drain()


def rows_sent(array, route):
    chunks, rows, lanes = array.shape
    shape = (chunks, 4, 4, 4, 2, rows // 128, lanes)
    copies = 13 * chunks + 10
    moved, maps = pl.pallas_call(
        rows_kernel,
        out_shape=(
            jax.ShapeDtypeStruct(shape, array.dtype),
            jax.ShapeDtypeStruct((4, 8) + route.shape, route.dtype),
        ),
        in_specs=[pl.BlockSpec(memory_space=pltpu.VMEM)] * 2,
        out_specs=(pl.BlockSpec(memory_space=pltpu.VMEM),) * 2,
        scratch_shapes=[
            pltpu.VMEM(shape, array.dtype),
            pltpu.VMEM(shape, array.dtype),
            pltpu.SemaphoreType.DMA((copies,)),
            pltpu.SemaphoreType.DMA((copies,)),
        ],
        compiler_params=pltpu.CompilerParams(collective_id=0, has_side_effects=True),
        name="rows_sent",
    )(array.reshape(shape), route)
    return moved.reshape(chunks, rows, lanes), maps


def cells_kernel(
    rows_ref,
    fine_ref,
    sharp_ref,
    mid_ref,
    map_ref,
    rebuilt_ref,
    fine_new_ref,
    mid_a_ref,
    mid_b_ref,
    coarse_ref,
    wide,
    back,
    sums,
):
    chunks, rows, lanes = rows_ref.shape
    cells = sharp_ref.shape[0]
    fine = fine_ref.shape[0] // cells
    width = fine_ref.shape[1]
    per_source = 2 * cells
    sources = rows // per_source
    for chunk in range(chunks):
        piece = rows_ref[chunk].astype(jnp.float32)
        wide[chunk] = jnp.where(piece > 0.5 * EMPTY, 0.0, piece)
        if chunk == 0:
            wide[chunks] = jnp.where(piece > 0.5 * EMPTY, 0.0, 1.0)
    for cell in range(cells):
        here = pl.ds(cell * fine, fine)
        centres = fine_ref[here, :]
        centres_wide = centres.astype(jnp.float32)
        norms = jnp.sum(centres_wide * centres_wide, axis=1, keepdims=True)
        lines = [pl.ds(cell * 2 + most, sources, stride=per_source) for most in range(2)]
        block = jnp.concatenate(
            [
                jnp.concatenate([wide[chunk, at, :] for at in lines], axis=0).astype(jnp.bfloat16)
                for chunk in range(chunks + 1)
            ],
            axis=1,
        )
        products = lax.dot_general(
            centres,
            block[:, :width],
            (((1,), (1,)), ((), ())),
            preferred_element_type=jnp.float32,
        )
        scores = (products - 0.5 * norms) * (sharp_ref[cell] / math.sqrt(width))
        exponent = jnp.exp(scores - jnp.max(scores, axis=0, keepdims=True))
        resp = (exponent / jnp.sum(exponent, axis=0, keepdims=True)).astype(jnp.bfloat16)
        weighted = jnp.dot(resp, block, preferred_element_type=jnp.float32)
        share = 1.0 / (weighted[:, width:] + 1.0)
        for chunk in range(chunks):
            at = slice(chunk * lanes, (chunk + 1) * lanes)
            fine_new_ref[here, pl.ds(chunk * lanes, lanes)] = (
                weighted[:, at] + centres_wide[:, at]
            ) * share
        sums[here, :] = weighted.astype(jnp.bfloat16)
        rebuilt = lax.dot_general(
            resp, centres, (((0,), (0,)), ((), ())), preferred_element_type=jnp.float32
        )
        for chunk in range(chunks):
            for most in range(2):
                back[chunk, lines[most], :] = rebuilt[
                    most * sources : (most + 1) * sources, chunk * lanes : (chunk + 1) * lanes
                ]
    for chunk in range(chunks):
        rebuilt_ref[chunk] = back[chunk].astype(jnp.bfloat16)
    step = 256
    split = mid_a_ref.shape[1]
    coarse_ref[...] = jnp.zeros_like(coarse_ref)
    for first in range(0, mid_a_ref.shape[0], step):
        place = lax.broadcasted_iota(jnp.int32, (step, rows), 0) + first
        picker = jnp.where(place == mid_ref[...], 1.0, 0.0).astype(jnp.bfloat16)
        part = jnp.dot(picker, sums[...], preferred_element_type=jnp.float32).astype(jnp.bfloat16)
        mid_a_ref[pl.ds(first, step), :] = part[:, :split]
        mid_b_ref[pl.ds(first, step), :] = part[:, split:]
        level = lax.broadcasted_iota(jnp.int32, (coarse_ref.shape[0], step), 0)
        route = jnp.where(level == map_ref[:, pl.ds(first, step)], 1.0, 0.0).astype(jnp.bfloat16)
        coarse_ref[...] += jnp.dot(route, part, preferred_element_type=jnp.float32)


def cells_done(rows, fine, sharpness, local_mid, mid_map, coarse_total, split):
    chunks, slots, lanes = rows.shape
    width = fine.shape[1]
    wide = width + lanes
    mids = mid_map.shape[1]
    vmem = pl.BlockSpec(memory_space=pltpu.VMEM)
    return pl.pallas_call(
        cells_kernel,
        out_shape=(
            jax.ShapeDtypeStruct((chunks, slots, lanes), jnp.bfloat16),
            jax.ShapeDtypeStruct((len(fine), width), jnp.float32),
            jax.ShapeDtypeStruct((mids, split), jnp.bfloat16),
            jax.ShapeDtypeStruct((mids, wide - split), jnp.bfloat16),
            jax.ShapeDtypeStruct((coarse_total, wide), jnp.float32),
        ),
        in_specs=[vmem, vmem, pl.BlockSpec(memory_space=pltpu.SMEM), vmem, vmem],
        out_specs=(vmem,) * 5,
        scratch_shapes=[
            pltpu.VMEM((chunks + 1, slots, lanes), jnp.float32),
            pltpu.VMEM((chunks, slots, lanes), jnp.float32),
            pltpu.VMEM((len(fine), wide), jnp.bfloat16),
        ],
        compiler_params=pltpu.CompilerParams(vmem_limit_bytes=48 * 1024 * 1024),
        name="cells_done",
    )(rows, fine, sharpness, local_mid, mid_map)


def sums_kernel(
    rows_ref,
    mid_a_ref,
    mid_b_ref,
    coarse_ref,
    out_ref,
    own_ref,
    total_ref,
    stage_a,
    stage_b,
    half_a,
    half_b,
    core_a,
    core_b,
    near_a,
    near_b,
    line_a,
    line_b,
    far_a,
    far_b,
    first_sum,
    second_sum,
    third_sum,
    send_sem,
    recv_sem,
):
    wires = Wires(send_sem, recv_sem)
    core = lax.axis_index(CORE)
    other = 1 - core
    greet(ring_peers(True))
    split = mid_a_ref.shape[-1]
    xs, zs, ys = Ring(wires, "member_0"), Ring(wires, "member_1"), Ring(wires, "group")
    xs_late, zs_late = Ring(wires, "member_0"), Ring(wires, "member_1")
    octet = Octet(wires)

    order_a = xs.order() + (xs.me,)
    order_b = zs.order() + (zs.me,)
    swap = wires.slots(8)
    for way in range(4):
        wires.send(
            mid_a_ref.at[order_a[way], :, other], core_a.at[order_a[way]], {CORE: other}, swap + way
        )
        wires.send(
            mid_b_ref.at[:, order_b[way], other],
            core_b.at[:, order_b[way]],
            {CORE: other},
            swap + 4 + way,
        )
    octet.start(lambda to: coarse_ref.at[to], first_sum.at[octet.me])
    first_sum[octet.me] = coarse_ref[octet.me]
    moving = Exchange(wires, (rows_ref, stage_a, stage_b, out_ref))
    moving.begin()

    xs.open()
    zs.open()
    for way in range(4):
        to = order_a[way]
        wires.arrived(core_a.at[to], {CORE: other}, swap + way)
        for z in range(4):
            half_a[to, z] = (
                mid_a_ref[to, z, core].astype(jnp.float32) + core_a[to, z].astype(jnp.float32)
            ).astype(jnp.bfloat16)
        if way < 3:
            xs.send(way, half_a.at[to], near_a.at[xs.me])
        to = order_b[way]
        wires.arrived(core_b.at[:, to], {CORE: other}, swap + 4 + way)
        for x in range(4):
            half_b[x, to] = (
                mid_b_ref[x, to, core].astype(jnp.float32) + core_b[x, to].astype(jnp.float32)
            ).astype(jnp.bfloat16)
        if way < 3:
            zs.send(way, half_b.at[:, to], near_b.at[zs.me])

    octet.finish(first_sum.at[octet.me])
    second_sum[zs.me] = sum(first_sum[at] for at in range(8))
    zs_coarse = Ring(wires, "member_1")
    zs_coarse.start(lambda to: second_sum.at[zs.me], second_sum.at[zs.me])

    moving.advance(0)

    zs_coarse.finish(second_sum.at[zs.me])
    third_sum[ys.me] = sum(second_sum[at] for at in range(4))
    ys.start(lambda to: third_sum.at[ys.me], third_sum.at[ys.me])

    xs.finish(near_a.at[xs.me])
    for z in range(4):
        line_a[z] = (
            half_a[xs.me, z].astype(jnp.float32)
            + sum(near_a[at, z].astype(jnp.float32) for at in xs.order())
        ).astype(jnp.bfloat16)
    zs_late.start(lambda to: line_a.at[to], far_a.at[zs.me])
    zs.finish(near_b.at[zs.me])
    for x in range(4):
        line_b[x] = (
            half_b[x, zs.me].astype(jnp.float32)
            + sum(near_b[at, x].astype(jnp.float32) for at in zs.order())
        ).astype(jnp.bfloat16)
    xs_late.start(lambda to: line_b.at[to], far_b.at[xs.me])

    moving.advance(1)

    ys.finish(third_sum.at[ys.me])
    total_ref[octet.me] = sum(third_sum[at] for at in range(4))
    octet.start(lambda to: total_ref.at[octet.me], total_ref.at[octet.me])

    zs_late.finish(far_a.at[zs.me])
    own_ref[:, pl.ds(0, split)] = line_a[zs.me].astype(jnp.float32) + sum(
        far_a[at].astype(jnp.float32) for at in zs.order()
    )
    xs_late.finish(far_b.at[xs.me])
    own_ref[:, pl.ds(split, mid_b_ref.shape[-1])] = line_b[xs.me].astype(jnp.float32) + sum(
        far_b[at].astype(jnp.float32) for at in xs.order()
    )
    moving.advance(2)
    octet.finish(total_ref.at[octet.me])
    wires.drain()


def sums_sent(array, mid_a, mid_b, coarse):
    chunks, rows, lanes = array.shape
    shape = (chunks, 4, 4, 4, 2, rows // 128, lanes)
    mid_dev = len(mid_a) // 32
    wide_a, wide_b = mid_a.shape[1], mid_b.shape[1]
    eighth = (len(coarse) // 8, coarse.shape[1])
    copies = 13 * chunks + 8 + 7 + 3 + 3 + 3 + 3 + 3 + 3 + 7
    vmem = pl.BlockSpec(memory_space=pltpu.VMEM)
    moved, own, total = pl.pallas_call(
        sums_kernel,
        out_shape=(
            jax.ShapeDtypeStruct(shape, array.dtype),
            jax.ShapeDtypeStruct((mid_dev, wide_a + wide_b), jnp.float32),
            jax.ShapeDtypeStruct((8,) + eighth, jnp.float32),
        ),
        in_specs=[vmem] * 4,
        out_specs=(vmem,) * 3,
        scratch_shapes=[
            pltpu.VMEM(shape, array.dtype),
            pltpu.VMEM(shape, array.dtype),
            pltpu.VMEM((4, 4, mid_dev, wide_a), jnp.bfloat16),
            pltpu.VMEM((4, 4, mid_dev, wide_b), jnp.bfloat16),
            pltpu.VMEM((4, 4, mid_dev, wide_a), jnp.bfloat16),
            pltpu.VMEM((4, 4, mid_dev, wide_b), jnp.bfloat16),
            pltpu.VMEM((4, 4, mid_dev, wide_a), jnp.bfloat16),
            pltpu.VMEM((4, 4, mid_dev, wide_b), jnp.bfloat16),
            pltpu.VMEM((4, mid_dev, wide_a), jnp.bfloat16),
            pltpu.VMEM((4, mid_dev, wide_b), jnp.bfloat16),
            pltpu.VMEM((4, mid_dev, wide_a), jnp.bfloat16),
            pltpu.VMEM((4, mid_dev, wide_b), jnp.bfloat16),
            pltpu.VMEM((8,) + eighth, jnp.float32),
            pltpu.VMEM((4,) + eighth, jnp.float32),
            pltpu.VMEM((4,) + eighth, jnp.float32),
            pltpu.SemaphoreType.DMA((copies,)),
            pltpu.SemaphoreType.DMA((copies,)),
        ],
        compiler_params=pltpu.CompilerParams(
            collective_id=1, has_side_effects=True, vmem_limit_bytes=56 * 1024 * 1024
        ),
        name="sums_sent",
    )(
        array.reshape(shape),
        mid_a.reshape(4, 4, 2, mid_dev, wide_a),
        mid_b.reshape(4, 4, 2, mid_dev, wide_b),
        coarse.reshape((8,) + eighth),
    )
    return moved.reshape(chunks, rows, lanes), own, total.reshape(coarse.shape)


def shards(
    samples,
    cell_of_row,
    fine_centroids,
    sharpness,
    mid_of_fine,
    mid_centroids,
    coarse_of_mid,
    coarse_centroids,
):
    groups = lax.axis_size("group")
    members = lax.axis_size(MEMBER)
    devices = groups * members
    row_count = samples.shape[0]
    feature_width = samples.shape[1]
    cell_dev = sharpness.shape[0]
    most_rows = 2 * row_count // (cell_dev * devices)
    total_cells = cell_dev * devices
    slots = total_cells * most_rows
    cell_ids = cell_of_row[:, 0]
    place = jnp.arange(row_count, dtype=jnp.int32)
    same = (cell_ids[:, None] == cell_ids[None, :]) & (place[:, None] < place[None, :])
    rank_in_cell = jnp.sum(same.astype(jnp.int32), axis=0)
    slot_index = cell_ids * most_rows + rank_in_cell
    picked = slot_index[None, :] == jnp.arange(slots, dtype=jnp.int32)[:, None]
    used = jnp.any(picked, axis=1)
    picked_rows = picked.astype(jnp.bfloat16)
    lanes = 128
    chunks = feature_width // lanes
    outgoing = jnp.einsum(
        "sr,rcw->csw",
        picked_rows,
        samples.reshape(row_count, chunks, lanes),
        preferred_element_type=jnp.float32,
    )
    outgoing = jnp.where(used[None, :, None], outgoing, EMPTY).astype(jnp.bfloat16)
    arrived, maps = rows_sent(outgoing, jnp.pad(coarse_of_mid, (0, lanes - len(coarse_of_mid)))[None])
    mid_dev = mid_centroids.shape[0]
    mid_group = mid_dev * members
    mid_map = maps.reshape(4, 4, 2, lanes)[..., :mid_dev].swapaxes(0, 1).reshape(1, mid_group)
    local_mid = (mid_of_fine - lax.axis_index("group") * mid_group)[None]
    coarse_total = coarse_centroids.shape[0]
    split = 4 * lanes
    rebuilt, fine_new, mid_a, mid_b, coarse_part = cells_done(
        arrived, fine_centroids, sharpness, local_mid, mid_map, coarse_total, split
    )
    returned, own, coarse_all = sums_sent(rebuilt, mid_a, mid_b, coarse_part)
    reconstruction = jnp.einsum(
        "sr,csw->rcw", picked_rows, returned, preferred_element_type=jnp.float32
    )
    reconstruction = reconstruction.astype(jnp.bfloat16).reshape(row_count, feature_width)
    own_sum, own_count = own[:, :feature_width], own[:, feature_width]
    mids_new = (own_sum + mid_centroids) / (own_count[:, None] + 1.0)
    coarse_sums, coarse_counts = coarse_all[:, :feature_width], coarse_all[:, feature_width]
    coarse_new = (coarse_sums + coarse_centroids) / (coarse_counts[:, None] + 1.0)
    return fine_new, mids_new, coarse_new, reconstruction


def solution(mesh):
    split = Mesh(
        mesh.devices.reshape(mesh.shape["group"], 4, 4, 2),
        ("group", "member_0", "member_1", "member_2"),
    )
    placed = (
        P(GROUP_MEMBER, None),
        P(GROUP_MEMBER, None),
        P(GROUP_MEMBER, None),
        P(GROUP_MEMBER),
        P(GROUP_MEMBER),
        P(GROUP_MEMBER, None),
        P(GROUP_MEMBER),
        P(),
    )
    return jax.shard_map(
        shards,
        mesh=split,
        in_specs=placed,
        out_specs=(P(GROUP_MEMBER, None), P(GROUP_MEMBER, None), P(), P(GROUP_MEMBER, None)),
        check_vma=False,
    )
```

time: 184 us -> 111 us (0.60)
  blocking collectives: 46.9 us -> 0 us
  Pallas kernels: 60.9 us -> 91.7 us
  matrix products: 18.7 us -> 3.28 us
  local copies, waits for them, and re-layouts: 25.8 us -> 10.7 us
  starting transfers between devices: 11.3 us -> 0 us
  other arithmetic: 11.7 us -> 3.75 us
  waiting for transfers between devices: 6.92 us -> 0 us
    all_to_all x4 -> x0, blocking collectives: 46.9 us -> none  [the longest x1 28 us: sum_in_two_steps(): lax.all_to_all(nearer.astype(jnp.bfloat16), far, split_axis=0, concat_axi...]
    pallas_call x2 -> x3, Pallas kernels: 60.9 us -> 91.7 us  [the longest x1 45.6 us: sums_sent(): pl.pallas_call(sums_kernel, out_shape=(jax.ShapeDtypeStruct(shape, array....]
    dot_general x4 -> x0, matrix products: 12.2 us -> none  [the longest x1 6.23 us: shards(): jnp.dot(picker.T, both, preferred_element_type=jnp.float32)]
    all_to_all x2 -> x0, starting transfers between devices: 11.3 us -> none  [the longest x1 6.03 us: copy_for_each(): return lax.all_to_all(copies, axis, split_axis=0, concat_axis=0, tiled=True)]
    reduce_sum x6 -> x0, other arithmetic: 7.46 us -> none  [the longest x1 2.95 us: sent_and_summed(): return arrived.astype(jnp.float32).sum(axis=0)]
    all_to_all x2 -> x0, waiting for transfers between devices: 6.92 us -> none  [the longest x1 6.92 us: copy_for_each(): return lax.all_to_all(copies, axis, split_axis=0, concat_axis=0, tiled=True)]
    reshape x3 -> x2, local copies, waits for them, and re-layouts: 7.8 us -> 1.8 us  [the longest x1 1.71 us: sums_sent(): moved.reshape(chunks, rows, lanes)]
    slice x5 -> x0, local copies, waits for them, and re-layouts: 4.76 us -> none  [the longest x2 4.41 us: shards(): jnp.dot(picker.T, both, preferred_element_type=jnp.float32)]
  transfers between devices with their start and end apart: 2 -> 0, of which waited for: 1 -> 0; matrix products, arithmetic and copies ran while one was open for 6% -> 0% of each run, Pallas kernels for 16% -> 0%
where the time goes in v2:
time: 111 us; the launch traced here: 110 us
  Pallas kernels  91.7 us (83%)
  local copies, waits for them, and re-layouts  10.7 us (10%)
  other arithmetic  3.75 us (3%)
  matrix products  3.28 us (3%)
    pallas_call x1, Pallas kernels, sums_sent(): pl.pallas_call(sums_kernel, out_shape=(jax.ShapeDtypeStruct(shape, array....  45.6 us
    pallas_call x1, Pallas kernels, rows_sent(): pl.pallas_call(rows_kernel, out_shape=(jax.ShapeDtypeStruct(shape, array....  34 us
    pallas_call x1, Pallas kernels, cells_done(): pl.pallas_call(cells_kernel, out_shape=(jax.ShapeDtypeStruct((chunks, slo...  12.1 us
    unnamed x20, local copies, waits for them, and re-layouts  6.98 us
    dot_general x1, matrix products, shards(): jnp.einsum('sr,rcw->csw', picked_rows, samples.reshape(row_count, chunks,...  2.26 us

profile of v2, /device:TPU:1, one launch (start us, length us, event | category | flops | bytes accessed | tf_op | source)
XLA Modules:
  0.0 110.2 jit_solution(15362814708440659434)
XLA Ops:
  0.6 1.2 %pad_bitcast_fusion.map_ref = s32[1,128]{1,0:T(1,128)} fusion(s32[64]{0:T(128)} %param.14), kind=kLoop, calls=%fused_computation.20 | loop fusion | bytes 768 | tf_op jit(solution)/shard_map/broadcast_in_dim | solution.py:539
  1.8 0.9 convert_reduce_fusion
  2.7 0.7 multiply_add_fusion
  3.4 0.3 fusion.2
  3.7 0.7 broadcast_subtract_fusion
  4.4 1.4 %copy.21 = bf16[512,768]{0,1:T(8,128)(2,1)S(1)} copy(bf16[512,768]{1,0:T(8,128)(2,1)} %param.8) | data formatting | bytes 1572864 | tf_op args[0]
  5.8 2.3 %select_convert_fusion = bf16[1024,6,128]{2,0,1:T(8,128)(2,1)} fusion(bf16[512,6,128]{0,2,1:T(8,128)(2,1)S(1)} %bitcast.41, pred[1024]{0:T(1024)(128)(4,1)S(1)} %fusion.2, s32[512]{0:T(512)S(1)} %multiply_add_fusion), kind=kOutput, calls=%fused_computation | convolution fusion | flops 807403520 | bytes 2362368 | tf_op jit(solution)/shard_map/sr,rcw->csw/dot_general | solution.py:532
  8.1 0.0 copy-start.4
  8.1 34.0 %rows_sent.1 = (bf16[6,4,4,4,2,8,128]{6,5,4,3,2,1,0:T(8,128)(2,1)}, s32[4,8,1,128]{3,2,1,0:T(1,128)}) custom-call(bf16[6,4,4,4,2,8,128]{6,5,4,3,2,1,0:T(8,128)(2,1)} %bitcast.38, s32[1,128]{1,0:T(1,128)} %pad_bitcast_fusion.map_ref), custom_call_target="tpu_custom_call" | custom-call | tf_op jit(solution)/shard_map/rows_sent/pallas_call | solution.py:209
  42.1 0.7 copy_bitcast_fusion
  42.8 0.1 reshape.58.map_ref
  42.9 0.0 copy-done.4
  42.9 0.0 copy-start
  42.9 1.4 %copy-done = bf16[6,4,4,4,2,8,128]{6,5,4,3,2,1,0:T(8,128)(2,1)S(1)} copy-done((bf16[6,4,4,4,2,8,128]{6,5,4,3,2,1,0:T(8,128)(2,1)S(1)}, bf16[6,4,4,4,2,8,128]{6,5,4,3,2,1,0:T(8,128)(2,1)}, u32[]{:S(2)}) %copy-start) | copy-done | bytes 1572888
  44.3 12.1 %cells_done.1 = (bf16[6,1024,128]{2,1,0:T(8,128)(2,1)S(1)}, f32[1024,768]{1,0:T(8,128)}, bf16[2048,512]{1,0:T(8,128)(2,1)}, bf16[2048,384]{1,0:T(8,128)(2,1)S(1)}, f32[64,896]{1,0:T(8,128)S(1)}) custom-call(bf16[6,1024,128]{2,1,0:T(8,128)(2,1)S(1)} %bitcast.30, bf16[1024,768]{1,0:T(8,128)(2,1)} %fine_ref.1, f32[4]{0:T(128)S(1)} %copy-done.4, ...), custom_call_target="tpu_custom_call" | custom-call | tf_op jit(solution)/shard_map/cells_done/pallas_call | solution.py:315
  56.4 0.0 copy-start.1
  56.4 1.1 %copy-done.1 = bf16[6,1024,128]{2,1,0:T(8,128)(2,1)} copy-done((bf16[6,1024,128]{2,1,0:T(8,128)(2,1)}, bf16[6,1024,128]{2,1,0:T(8,128)(2,1)S(1)}, u32[]{:S(2)}) %copy-start.1) | copy-done | bytes 1572888
  57.5 0.0 copy-start.2
  57.5 1.2 %copy-done.2 = bf16[2048,384]{1,0:T(8,128)(2,1)} copy-done((bf16[2048,384]{1,0:T(8,128)(2,1)}, bf16[2048,384]{1,0:T(8,128)(2,1)S(1)}, u32[]{:S(2)}) %copy-start.2) | copy-done | bytes 1572888
  58.7 0.0 copy-start.3
  58.7 0.7 copy-done.3
  59.4 45.6 %sums_sent.1 = (bf16[6,4,4,4,2,8,128]{6,5,4,3,2,1,0:T(8,128)(2,1)}, f32[64,896]{1,0:T(8,128)}, f32[8,8,896]{2,1,0:T(8,128)}) custom-call(bf16[6,4,4,4,2,8,128]{6,5,4,3,2,1,0:T(8,128)(2,1)} %bitcast.31, bf16[4,4,2,64,512]{4,3,2,1,0:T(8,128)(2,1)} %bitcast.36, bf16[4,4,2,64,384]{4,3,2,1,0:T(8,128)(2,1)} %bitcast.32, f32[8,8,896]{2,1,0:T(8,128)} %bitcast.33), custom_call_target="tpu_custom_call" | custom-call | tf_op jit(solution)/shard_map/sums_sent/pallas_call | solution.py:462
  105.0 1.7 %copy.24 = bf16[6,1024,128]{1,2,0:T(8,128)(2,1)S(1)} copy(bf16[6,1024,128]{2,1,0:T(8,128)(2,1)} %bitcast.37) | data formatting | bytes 3145728 | tf_op jit(solution)/shard_map/reshape | solution.py:500
  106.7 1.0 fusion
  107.8 0.0 copy-start.6
  107.8 0.0 copy-start.5
  107.8 0.0 copy-start.7
  107.8 0.0 copy-start.8
  107.8 0.1 convert_element_type.16
  107.9 1.2 %copy.25 = bf16[512,768]{1,0:T(8,128)(2,1)} copy(bf16[512,768]{0,1:T(8,128)(2,1)S(1)} %bitcast.35) | data formatting | bytes 1572864
  109.1 0.0 copy-done.6
  109.1 0.1 fusion.11
  109.2 0.0 copy-done.5
  109.2 0.1 add_reduce_fusion
  109.3 0.0 copy-done.7
  109.3 0.0 copy-done.8
  109.3 0.8 fusion.10
Async XLA Ops:
  8.1 34.9 %copy-start.4 = (f32[4]{0:T(128)S(1)}, f32[4]{0:T(128)}, u32[]{:S(2)}) copy-start(f32[4]{0:T(128)} %sharp_ref.1) | copy-start | bytes 52
  42.9 1.4 %copy-start = (bf16[6,4,4,4,2,8,128]{6,5,4,3,2,1,0:T(8,128)(2,1)S(1)}, bf16[6,4,4,4,2,8,128]{6,5,4,3,2,1,0:T(8,128)(2,1)}, u32[]{:S(2)}) copy-start(bf16[6,4,4,4,2,8,128]{6,5,4,3,2,1,0:T(8,128)(2,1)} %get-tuple-element.14) | copy-start | bytes 4718596
  56.4 1.1 %copy-start.1 = (bf16[6,1024,128]{2,1,0:T(8,128)(2,1)}, bf16[6,1024,128]{2,1,0:T(8,128)(2,1)S(1)}, u32[]{:S(2)}) copy-start(bf16[6,1024,128]{2,1,0:T(8,128)(2,1)S(1)} %get-tuple-element.17) | copy-start | bytes 4718596
  57.5 1.2 %copy-start.2 = (bf16[2048,384]{1,0:T(8,128)(2,1)}, bf16[2048,384]{1,0:T(8,128)(2,1)S(1)}, u32[]{:S(2)}) copy-start(bf16[2048,384]{1,0:T(8,128)(2,1)S(1)} %get-tuple-element.19) | copy-start | bytes 4718596
  58.7 0.7 copy-start.3
  107.8 1.3 %copy-start.6 = (f32[8,8,896]{2,1,0:T(8,128)S(1)}, f32[8,8,896]{2,1,0:T(8,128)}, u32[]{:S(2)}) copy-start(f32[8,8,896]{2,1,0:T(8,128)} %get-tuple-element.22) | copy-start | bytes 688132
  107.8 1.4 %copy-start.5 = (f32[64,896]{1,0:T(8,128)S(1)}, f32[64,896]{1,0:T(8,128)}, u32[]{:S(2)}) copy-start(f32[64,896]{1,0:T(8,128)} %get-tuple-element.21) | copy-start | bytes 688132
  107.8 1.5 %copy-start.7 = (f32[64,768]{1,0:T(8,128)S(1)}, f32[64,768]{1,0:T(8,128)}, u32[]{:S(2)}) copy-start(f32[64,768]{1,0:T(8,128)} %param.15) | copy-start | bytes 589828
  107.8 1.5 %copy-start.8 = (f32[64,768]{1,0:T(8,128)S(1)}, f32[64,768]{1,0:T(8,128)}, u32[]{:S(2)}) copy-start(f32[64,768]{1,0:T(8,128)} %param.13) | copy-start | bytes 589828

commit v3 on v1

v3 whole, which is shorter than its diff:
```python
import math

import jax
import jax.numpy as jnp
from jax import lax
from jax.experimental import pallas as pl
from jax.experimental.pallas import tpu as pltpu
from jax.sharding import Mesh
from jax.sharding import PartitionSpec as P

MEMBER = ("member_0", "member_1", "member_2")
GROUP_MEMBER = ("group", "member_0", "member_1", "member_2")
RINGS = ("group", "member_0", "member_1")
CORE = "member_2"
EMPTY = 64.0
MESH_ID = pl.DeviceIdType.MESH


class Wires:
    def __init__(self, send_sem, recv_sem):
        self.send_sem, self.recv_sem = send_sem, recv_sem
        self.sent, self.arrivals, self.last = 0, 0, []

    def slots(self, number):
        self.arrivals += number
        return self.arrivals - number

    def copy(self, source, target, to, send_at, recv_at):
        return pltpu.make_async_remote_copy(
            src_ref=source,
            dst_ref=target,
            send_sem=self.send_sem.at[send_at],
            recv_sem=self.recv_sem.at[recv_at],
            device_id=to,
            device_id_type=MESH_ID,
        )

    def send(self, source, target, to, recv_at):
        copy = self.copy(source, target, to, self.sent, recv_at)
        self.sent += 1
        copy.start()
        self.last.append(copy)

    def arrived(self, like, to, recv_at):
        self.copy(like, like, to, 0, recv_at).wait_recv()

    def drain(self):
        for copy in self.last:
            copy.wait_send()


def greet(peers):
    barrier = pltpu.get_barrier_semaphore()
    for peer in peers:
        pl.semaphore_signal(barrier, inc=1, device_id=peer, device_id_type=MESH_ID)
    pl.semaphore_wait(barrier, len(peers))


def ring_places(axis):
    me = lax.axis_index(axis)
    return me, lax.rem(me + 1, 4), lax.rem(me + 3, 4), lax.rem(me + 2, 4)


def ring_peers(both_cores):
    core = lax.axis_index(CORE)
    peers = [{CORE: 1 - core}]
    for axis in RINGS:
        for to in ring_places(axis)[1:]:
            peers.append({axis: to})
            if both_cores:
                peers.append({axis: to, CORE: 1 - core})
    return peers


class Exchange:
    def __init__(self, wires, refs):
        self.wires, self.refs = wires, refs
        self.core = lax.axis_index(CORE)
        self.rings = [ring_places(axis) for axis in RINGS]
        self.chunks = range(refs[0].shape[0])
        self.running = [None] * len(self.chunks)

    def spot(self, chunk, dim, index, core_at=slice(None)):
        at = [chunk, slice(None), slice(None), slice(None), core_at]
        at[dim + 1] = index
        return tuple(at)

    def start(self, phase, chunk):
        wires, core, other = self.wires, self.core, 1 - self.core
        dim = (chunk + phase) % 3
        source, target = self.refs[phase], self.refs[phase + 1]
        axis = RINGS[dim]
        me, up, down, across = self.rings[dim]
        if phase < 2:
            base = wires.slots(3)
            for way, to in enumerate((across, up, down)):
                wires.send(
                    source.at[self.spot(chunk, dim, to)],
                    target.at[self.spot(chunk, dim, me)],
                    {axis: to},
                    base + way,
                )
            own = self.spot(chunk, dim, me)
        else:
            base = wires.slots(7)
            for way, to in enumerate((across, up, down)):
                for core_at in (0, 1):
                    wires.send(
                        source.at[self.spot(chunk, dim, to, core_at)],
                        target.at[self.spot(chunk, dim, me, core)],
                        {axis: to, CORE: core_at},
                        base + 2 * way + core,
                    )
            wires.send(
                source.at[self.spot(chunk, dim, me, other)],
                target.at[self.spot(chunk, dim, me, core)],
                {CORE: other},
                base + 6,
            )
            own = self.spot(chunk, dim, me, core)
        target[own] = source[own]
        self.running[chunk] = base

    def finish(self, phase, chunk):
        dim = (chunk + phase) % 3
        me, up, _, _ = self.rings[dim]
        if phase < 2:
            like, number = self.refs[phase + 1].at[self.spot(chunk, dim, me)], 3
        else:
            like, number = self.refs[phase + 1].at[self.spot(chunk, dim, me, self.core)], 7
        for at in range(number):
            self.wires.arrived(like, {RINGS[dim]: up}, self.running[chunk] + at)

    def begin(self):
        for chunk in self.chunks:
            self.start(0, chunk)

    def advance(self, phase):
        for chunk in self.chunks:
            self.finish(phase, chunk)
            if phase < 2:
                self.start(phase + 1, chunk)


class Octet:
    def __init__(self, wires):
        self.wires = wires
        self.me = lax.axis_index("member_0") * 2 + lax.axis_index(CORE)

    def start(self, source_of, target):
        self.base = self.wires.slots(7)
        for step in range(1, 8):
            to = lax.rem(self.me + step, 8)
            where = {"member_0": to // 2, CORE: lax.rem(to, 2)}
            self.wires.send(source_of(to), target, where, self.base + step - 1)

    def finish(self, like):
        for step in range(7):
            self.wires.arrived(like, {CORE: 1 - lax.axis_index(CORE)}, self.base + step)


class Ring:
    def __init__(self, wires, axis):
        self.wires, self.axis = wires, axis
        self.me, self.up, self.down, self.across = ring_places(axis)

    def order(self):
        return (self.across, self.up, self.down)

    def open(self):
        self.base = self.wires.slots(3)

    def send(self, way, source, target):
        self.wires.send(source, target, {self.axis: self.order()[way]}, self.base + way)

    def start(self, source_of, target):
        self.open()
        for way, to in enumerate(self.order()):
            self.send(way, source_of(to), target)

    def finish(self, like):
        for way in range(3):
            self.wires.arrived(like, {self.axis: self.up}, self.base + way)


def diagonal(rows, lanes):
    return lax.broadcasted_iota(jnp.int32, (rows, lanes), 0) == lax.broadcasted_iota(
        jnp.int32, (rows, lanes), 1
    )


def as_column(row, rows):
    return jnp.sum(
        jnp.where(diagonal(rows, row.shape[1]), row, jnp.zeros_like(row)), axis=1, keepdims=True
    )


def step_kernel(
    samples_ref,
    cell_ref,
    fine_ref,
    sharp_ref,
    mid_ref,
    mids_ref,
    route_ref,
    coarse_ref,
    fine_new_ref,
    mids_new_ref,
    coarse_new_ref,
    rec_ref,
    outgoing,
    there_a,
    there_b,
    arrived,
    rebuilt,
    back_a,
    back_b,
    returned,
    wide,
    back,
    resps,
    sums,
    chosen,
    maps,
    give,
    core_in,
    half_a,
    half_b,
    near_a,
    near_b,
    line_a,
    line_b,
    far_a,
    far_b,
    give_m,
    core_m,
    half_m,
    near_m,
    line_m,
    far_m,
    part_c,
    first_sum,
    second_sum,
    third_sum,
    total,
    send_sem,
    recv_sem,
):
    f32, bf16 = jnp.float32, jnp.bfloat16
    wires = Wires(send_sem, recv_sem)
    core = lax.axis_index(CORE)
    other = 1 - core
    chunks, lanes = outgoing.shape[0], outgoing.shape[-1]
    row_count, width = samples_ref.shape
    slots = chosen.shape[1]
    cells = sharp_ref.shape[0]
    fine = fine_ref.shape[0] // cells
    per_source = 2 * cells
    sources = slots // per_source
    mid_dev = mids_ref.shape[0]
    split = half_a.shape[-1]

    cell_row = cell_ref[...]
    cell_column = as_column(cell_row, row_count)
    earlier = lax.broadcasted_iota(jnp.int32, (row_count, row_count), 0) < lax.broadcasted_iota(
        jnp.int32, (row_count, row_count), 1
    )
    rank = jnp.sum(
        jnp.where((cell_column == cell_row) & earlier, 1, 0), axis=0, keepdims=True
    )
    slot_row = cell_row * 2 + rank
    place = lax.broadcasted_iota(jnp.int32, (slots, row_count), 0)
    picked = jnp.where(place == slot_row, 1.0, 0.0).astype(bf16)
    used = jnp.dot(picked, jnp.ones((row_count, lanes), bf16), preferred_element_type=f32) > 0.5

    greet(ring_peers(True))
    moving = Exchange(wires, (outgoing, there_a, there_b, arrived))
    for chunk in range(chunks):
        lines = jnp.dot(
            picked, samples_ref[:, pl.ds(chunk * lanes, lanes)], preferred_element_type=f32
        )
        lines = jnp.where(used, lines, EMPTY)
        outgoing[chunk] = lines.reshape(outgoing.shape[1:]).astype(bf16)
        moving.start(0, chunk)
    octet = Octet(wires)
    xs, zs, ys = Ring(wires, "member_0"), Ring(wires, "member_1"), Ring(wires, "group")
    maps_ring = Ring(wires, "member_1")
    octet.start(lambda to: route_ref, maps.at[zs.me, octet.me])
    maps[zs.me, octet.me] = route_ref[...]
    slot_column = as_column(slot_row, row_count)
    along = lax.broadcasted_iota(jnp.int32, (row_count, slots), 1)
    chosen[...] = jnp.where(along == slot_column, 1.0, 0.0).astype(bf16)
    octet.finish(maps.at[zs.me, octet.me])
    maps_ring.start(lambda to: maps.at[zs.me], maps.at[zs.me])
    moving.advance(0)
    maps_ring.finish(maps.at[zs.me])
    moving.advance(1)
    moving.advance(2)

    for chunk in range(chunks):
        piece = arrived[chunk].astype(f32).reshape(slots, lanes)
        wide[chunk] = jnp.where(piece > 0.5 * EMPTY, 0.0, piece)
        if chunk == 0:
            wide[chunks] = jnp.where(piece > 0.5 * EMPTY, 0.0, 1.0)

    def cell_rows(cell, number):
        spots = [pl.ds(cell * 2 + most, sources, stride=per_source) for most in range(2)]
        return jnp.concatenate(
            [
                jnp.concatenate([wide[chunk, at, :] for at in spots], axis=0).astype(bf16)
                for chunk in range(number)
            ],
            axis=1,
        )

    for cell in range(cells):
        centres = fine_ref[pl.ds(cell * fine, fine), :]
        centres_wide = centres.astype(f32)
        norms = jnp.sum(centres_wide * centres_wide, axis=1, keepdims=True)
        products = lax.dot_general(
            centres,
            cell_rows(cell, chunks),
            (((1,), (1,)), ((), ())),
            preferred_element_type=f32,
        )
        scores = (products - 0.5 * norms) * (sharp_ref[cell] / math.sqrt(width))
        exponent = jnp.exp(scores - jnp.max(scores, axis=0, keepdims=True))
        resp = (exponent / jnp.sum(exponent, axis=0, keepdims=True)).astype(bf16)
        resps[cell] = resp
        lines = lax.dot_general(resp, centres, (((0,), (0,)), ((), ())), preferred_element_type=f32)
        for chunk in range(chunks):
            for most in range(2):
                back[chunk, pl.ds(cell * 2 + most, sources, stride=per_source), :] = lines[
                    most * sources : (most + 1) * sources, chunk * lanes : (chunk + 1) * lanes
                ]
    homing = Exchange(wires, (rebuilt, back_a, back_b, returned))
    for chunk in range(chunks):
        rebuilt[chunk] = back[chunk].reshape(rebuilt.shape[1:]).astype(bf16)
        homing.start(0, chunk)

    for cell in range(cells):
        here = pl.ds(cell * fine, fine)
        weighted = jnp.dot(resps[cell], cell_rows(cell, chunks + 1), preferred_element_type=f32)
        sums[here, :] = weighted.astype(bf16)
        centres_wide = fine_ref[here, :].astype(f32)
        share = 1.0 / (weighted[:, width:] + 1.0)
        for chunk in range(chunks):
            at = slice(chunk * lanes, (chunk + 1) * lanes)
            fine_new_ref[here, pl.ds(chunk * lanes, lanes)] = (
                weighted[:, at] + centres_wide[:, at]
            ) * share

    rows_of = 4 * mid_dev
    local_mid = mid_ref[...] - lax.axis_index("group") * (32 * mid_dev)
    spread = lax.broadcasted_iota(jnp.int32, (rows_of, fine_ref.shape[0]), 0)
    spread = (spread // mid_dev) * (2 * mid_dev) + spread % mid_dev

    def mid_part(x, core_at):
        wanted = local_mid - (x * 8 + core_at) * mid_dev
        picker = jnp.where(spread == wanted, 1.0, 0.0).astype(bf16)
        return jnp.dot(picker, sums[...], preferred_element_type=f32)

    def mass_row(part, z):
        tile = part[z * mid_dev : (z + 1) * mid_dev, width:]
        return jnp.sum(
            jnp.where(diagonal(mid_dev, lanes), tile, 0.0), axis=0, keepdims=True
        )

    order_x = xs.order() + (xs.me,)
    swap, swap_m = wires.slots(4), wires.slots(4)
    for way, x in enumerate(order_x):
        part = mid_part(x, other)
        for z in range(4):
            give[x, z] = part[z * mid_dev : (z + 1) * mid_dev, :width].astype(bf16)
            give_m[x, z] = mass_row(part, z)
        wires.send(give.at[x], core_in.at[x], {CORE: other}, swap + way)
        wires.send(give_m.at[x], core_m.at[x], {CORE: other}, swap_m + way)
    xs_m = Ring(wires, "member_0")
    xs.open()
    xs_m.open()
    level = lax.broadcasted_iota(jnp.int32, (coarse_ref.shape[0], lanes), 0)
    coarse_part = jnp.zeros((coarse_ref.shape[0], width), f32)
    coarse_mass = jnp.zeros((coarse_ref.shape[0], lanes), f32)
    for way, x in enumerate(order_x):
        part = mid_part(x, core)
        wires.arrived(core_in.at[x], {CORE: other}, swap + way)
        wires.arrived(core_m.at[x], {CORE: other}, swap_m + way)
        for z in range(4):
            half = part[z * mid_dev : (z + 1) * mid_dev, :width] + core_in[x, z].astype(f32)
            half = half.astype(bf16)
            half_a[x, z] = half[:, :split]
            half_b[z, x] = half[:, split:]
            masses = mass_row(part, z) + core_m[x, z]
            half_m[x, z] = masses
            goes = level == maps[z, x * 2 + core]
            coarse_mass += jnp.where(goes, masses, 0.0)
            coarse_part += jnp.dot(
                jnp.where(goes, 1.0, 0.0).astype(bf16)[:, :mid_dev],
                half,
                preferred_element_type=f32,
            )
        if way < 3:
            xs.send(way, half_a.at[x], near_a.at[xs.me])
            xs_m.send(way, half_m.at[x], near_m.at[xs.me])
    zs.start(lambda to: half_b.at[to], near_b.at[zs.me])
    coarse_mass = jnp.broadcast_to(jnp.sum(coarse_mass, axis=1, keepdims=True), coarse_mass.shape)
    for at in range(8):
        part_c[at, :, pl.ds(0, width)] = coarse_part[8 * at : 8 * at + 8]
        part_c[at, :, pl.ds(width, lanes)] = coarse_mass[8 * at : 8 * at + 8]
    octet.start(lambda to: part_c.at[to], first_sum.at[octet.me])
    first_sum[octet.me] = part_c[octet.me]

    homing.advance(0)

    octet.finish(first_sum.at[octet.me])
    second_sum[zs.me] = sum(first_sum[at] for at in range(8))
    zs_coarse = Ring(wires, "member_1")
    zs_coarse.start(lambda to: second_sum.at[zs.me], second_sum.at[zs.me])

    xs.finish(near_a.at[xs.me])
    xs_m.finish(near_m.at[xs.me])
    for z in range(4):
        line_a[z] = (
            half_a[xs.me, z].astype(f32) + sum(near_a[at, z].astype(f32) for at in xs.order())
        ).astype(bf16)
        line_m[z] = half_m[xs.me, z] + sum(near_m[at, z] for at in xs.order())
    zs_late, zs_m, xs_late = Ring(wires, "member_1"), Ring(wires, "member_1"), Ring(wires, "member_0")
    zs_late.start(lambda to: line_a.at[to], far_a.at[zs.me])
    zs_m.start(lambda to: line_m.at[to], far_m.at[zs.me])
    zs.finish(near_b.at[zs.me])
    for x in range(4):
        line_b[x] = (
            half_b[zs.me, x].astype(f32) + sum(near_b[at, x].astype(f32) for at in zs.order())
        ).astype(bf16)
    xs_late.start(lambda to: line_b.at[to], far_b.at[xs.me])

    zs_coarse.finish(second_sum.at[zs.me])
    third_sum[ys.me] = sum(second_sum[at] for at in range(4))
    ys.start(lambda to: third_sum.at[ys.me], third_sum.at[ys.me])

    homing.advance(1)

    ys.finish(third_sum.at[ys.me])
    total[octet.me] = sum(third_sum[at] for at in range(4))
    octet.start(lambda to: total.at[octet.me], total.at[octet.me])

    zs_late.finish(far_a.at[zs.me])
    zs_m.finish(far_m.at[zs.me])
    xs_late.finish(far_b.at[xs.me])
    masses = line_m[zs.me] + sum(far_m[at] for at in zs.order())
    share = 1.0 / (as_column(masses, mid_dev) + 1.0)
    own_a = line_a[zs.me].astype(f32) + sum(far_a[at].astype(f32) for at in zs.order())
    own_b = line_b[xs.me].astype(f32) + sum(far_b[at].astype(f32) for at in xs.order())
    mids_new_ref[:, pl.ds(0, split)] = (own_a + mids_ref[:, pl.ds(0, split)]) * share
    mids_new_ref[:, pl.ds(split, split)] = (own_b + mids_ref[:, pl.ds(split, split)]) * share

    octet.finish(total.at[octet.me])
    for at in range(8):
        here = pl.ds(8 * at, 8)
        share = 1.0 / (total[at, :, pl.ds(width, lanes)] + 1.0)
        for chunk in range(chunks):
            there = pl.ds(chunk * lanes, lanes)
            coarse_new_ref[here, there] = (total[at, :, there] + coarse_ref[here, there]) * share
    for chunk in range(chunks):
        homing.finish(2, chunk)
        lines = returned[chunk].astype(f32).reshape(slots, lanes).astype(bf16)
        rec_ref[:, pl.ds(chunk * lanes, lanes)] = jnp.dot(
            chosen[...], lines, preferred_element_type=f32
        ).astype(bf16)
    wires.drain()


def shards(
    samples,
    cell_of_row,
    fine_centroids,
    sharpness,
    mid_of_fine,
    mid_centroids,
    coarse_of_mid,
    coarse_centroids,
):
    row_count, width = samples.shape
    cells = sharpness.shape[0]
    fine_total = fine_centroids.shape[0]
    fine = fine_total // cells
    mid_dev = mid_centroids.shape[0]
    coarse_total = coarse_centroids.shape[0]
    lanes = 128
    chunks = width // lanes
    slots = 128 * 2 * cells
    split = width // 2
    moved = (chunks, 4, 4, 4, 2, 2 * cells, lanes)
    eighth = (coarse_total // 8, width + lanes)
    copies = 2 * 13 * chunks + 3 * 7 + 9 * 3 + 8
    f32, bf16 = jnp.float32, jnp.bfloat16
    vmem = pl.BlockSpec(memory_space=pltpu.VMEM)
    return pl.pallas_call(
        step_kernel,
        out_shape=(
            jax.ShapeDtypeStruct((fine_total, width), f32),
            jax.ShapeDtypeStruct((mid_dev, width), f32),
            jax.ShapeDtypeStruct((coarse_total, width), f32),
            jax.ShapeDtypeStruct((row_count, width), bf16),
        ),
        in_specs=[vmem, vmem, vmem, pl.BlockSpec(memory_space=pltpu.SMEM)] + [vmem] * 4,
        out_specs=(vmem,) * 4,
        scratch_shapes=[pltpu.VMEM(moved, bf16)] * 8
        + [
            pltpu.VMEM((chunks + 1, slots, lanes), f32),
            pltpu.VMEM((chunks, slots, lanes), f32),
            pltpu.VMEM((cells, fine, 2 * 128), bf16),
            pltpu.VMEM((fine_total, width + lanes), bf16),
            pltpu.VMEM((row_count, slots), bf16),
            pltpu.VMEM((4, 8, 1, lanes), jnp.int32),
            pltpu.VMEM((4, 4, mid_dev, width), bf16),
            pltpu.VMEM((4, 4, mid_dev, width), bf16),
        ]
        + [pltpu.VMEM((4, 4, mid_dev, split), bf16)] * 4
        + [pltpu.VMEM((4, mid_dev, split), bf16)] * 4
        + [pltpu.VMEM((4, 4, 1, lanes), f32)] * 4
        + [pltpu.VMEM((4, 1, lanes), f32)] * 2
        + [pltpu.VMEM((8,) + eighth, f32)] * 2
        + [pltpu.VMEM((4,) + eighth, f32)] * 2
        + [
            pltpu.VMEM((8,) + eighth, f32),
            pltpu.SemaphoreType.DMA((copies,)),
            pltpu.SemaphoreType.DMA((copies,)),
        ],
        compiler_params=pltpu.CompilerParams(
            collective_id=0, has_side_effects=True, vmem_limit_bytes=60 * 1024 * 1024
        ),
        name="lloyd_step",
    )(
        samples,
        cell_of_row.reshape(1, row_count),
        fine_centroids,
        sharpness,
        mid_of_fine.reshape(1, fine_total),
        mid_centroids,
        jnp.pad(coarse_of_mid, (0, lanes - mid_dev))[None],
        coarse_centroids,
    )


def solution(mesh):
    split = Mesh(
        mesh.devices.reshape(mesh.shape["group"], 4, 4, 2),
        ("group", "member_0", "member_1", "member_2"),
    )
    placed = (
        P(GROUP_MEMBER, None),
        P(GROUP_MEMBER, None),
        P(GROUP_MEMBER, None),
        P(GROUP_MEMBER),
        P(GROUP_MEMBER),
        P(GROUP_MEMBER, None),
        P(GROUP_MEMBER),
        P(),
    )
    return jax.shard_map(
        shards,
        mesh=split,
        in_specs=placed,
        out_specs=(P(GROUP_MEMBER, None), P(GROUP_MEMBER, None), P(), P(GROUP_MEMBER, None)),
        check_vma=False,
    )
```

time: 184 us -> 92.3 us (0.50)
  blocking collectives: 46.9 us -> 0 us
  Pallas kernels: 60.9 us -> 84.2 us
  matrix products: 18.7 us -> 0 us
  local copies, waits for them, and re-layouts: 25.8 us -> 7.26 us
  other arithmetic: 11.7 us -> 0 us
  starting transfers between devices: 11.3 us -> 0 us
  waiting for transfers between devices: 6.92 us -> 0 us
    all_to_all x4 -> x0, blocking collectives: 46.9 us -> none  [the longest x1 28 us: sum_in_two_steps(): lax.all_to_all(nearer.astype(jnp.bfloat16), far, split_axis=0, concat_axi...]
    pallas_call x2 -> x1, Pallas kernels: 60.9 us -> 84.2 us  [shards(): pl.pallas_call(step_kernel, out_shape=(jax.ShapeDtypeStruct((fine_total,...]
    dot_general x5 -> x0, matrix products: 14.4 us -> none  [the longest x1 6.23 us: shards(): jnp.dot(picker.T, both, preferred_element_type=jnp.float32)]
    all_to_all x2 -> x0, starting transfers between devices: 11.3 us -> none  [the longest x1 6.03 us: copy_for_each(): return lax.all_to_all(copies, axis, split_axis=0, concat_axis=0, tiled=True)]
    reduce_sum x7 -> x0, other arithmetic: 8.39 us -> none  [the longest x1 2.95 us: sent_and_summed(): return arrived.astype(jnp.float32).sum(axis=0)]
    reshape x3 -> x0, local copies, waits for them, and re-layouts: 7.8 us -> none  [the longest x1 3.38 us: shards(): rebuilt.reshape(cell_dev, devices, most_rows, chunks, lanes)]
    all_to_all x2 -> x0, waiting for transfers between devices: 6.92 us -> none  [the longest x1 6.92 us: copy_for_each(): return lax.all_to_all(copies, axis, split_axis=0, concat_axis=0, tiled=True)]
    transpose x3 -> x0, local copies, waits for them, and re-layouts: 4.77 us -> none  [the longest x2 2.41 us: split_up(): return jnp.moveaxis(pieces, dim, 0)]
  transfers between devices with their start and end apart: 2 -> 0, of which waited for: 1 -> 0; matrix products, arithmetic and copies ran while one was open for 6% -> 0% of each run, Pallas kernels for 16% -> 0%
where the time goes in v3:
time: 92.3 us; the launch traced here: 92.1 us
  Pallas kernels  84.2 us (91%)
  local copies, waits for them, and re-layouts  7.26 us (8%)
    pallas_call x1, Pallas kernels, shards(): pl.pallas_call(step_kernel, out_shape=(jax.ShapeDtypeStruct((fine_total,...  84.2 us
    unnamed x10, local copies, waits for them, and re-layouts  6.1 us

profile of v3, /device:TPU:1, one launch (start us, length us, event | category | flops | bytes accessed | tf_op | source)
XLA Modules:
  0.0 92.1 jit_solution(8119389979779466986)
XLA Ops:
  0.6 1.2 %pad_bitcast_fusion.route_ref = s32[1,128]{1,0:T(1,128)} fusion(s32[64]{0:T(128)} %param.14), kind=kLoop, calls=%fused_computation | loop fusion | bytes 768 | tf_op jit(solution)/shard_map/broadcast_in_dim | solution.py:541
  1.8 84.2 %lloyd_step.1 = (f32[1024,768]{1,0:T(8,128)}, f32[64,768]{1,0:T(8,128)}, f32[64,768]{1,0:T(8,128)}, bf16[512,768]{1,0:T(8,128)(2,1)}) custom-call(bf16[512,768]{1,0:T(8,128)(2,1)} %samples_ref.1, s32[1,512]{1,0:T(1,128)} %bitcast.5, bf16[1024,768]{1,0:T(8,128)(2,1)} %fine_ref.1, f32[4]{0:T(128)} %sharp_ref.1, s32[1,1024]{1,0:T(1,128)} %bitcast.4, ...), custom_call_target="tpu_custom_call" | custom-call | tf_op jit(solution)/shard_map/lloyd_step/pallas_call | solution.py:498
  86.0 0.0 copy-start.2
  86.0 0.0 copy-start.1
  86.0 0.0 copy-start
  86.0 3.8 %copy.16 = f32[1024,768]{1,0:T(8,128)} copy(f32[1024,768]{1,0:T(8,128)} %get-tuple-element.8) | data formatting | bytes 6291456
  89.9 0.0 copy-done.2
  89.9 0.7 copy.17
  90.5 0.0 copy-done.1
  90.5 0.7 copy.18
  91.2 0.0 copy-done
  91.2 0.9 copy.19
Async XLA Ops:
  86.0 3.9 %copy-start.2 = (f32[64,768]{1,0:T(8,128)S(1)}, f32[64,768]{1,0:T(8,128)}, u32[]{:S(2)}) copy-start(f32[64,768]{1,0:T(8,128)} %get-tuple-element.9) | copy-start | bytes 589828
  86.0 4.6 %copy-start.1 = (f32[64,768]{1,0:T(8,128)S(1)}, f32[64,768]{1,0:T(8,128)}, u32[]{:S(2)}) copy-start(f32[64,768]{1,0:T(8,128)} %get-tuple-element.10) | copy-start | bytes 589828
  86.0 5.2 %copy-start = (bf16[512,768]{1,0:T(8,128)(2,1)S(1)}, bf16[512,768]{1,0:T(8,128)(2,1)}, u32[]{:S(2)}) copy-start(bf16[512,768]{1,0:T(8,128)(2,1)} %get-tuple-element.11) | copy-start | bytes 2359300

commit v4 on v3

--- a/solution.py
+++ b/solution.py
@@ -19,11 +19,16 @@
 class Wires:
     def __init__(self, send_sem, recv_sem):
         self.send_sem, self.recv_sem = send_sem, recv_sem
-        self.sent, self.arrivals, self.last = 0, 0, []
-
-    def slots(self, number):
-        self.arrivals += number
-        return self.arrivals - number
+        self.arrivals, self.leave = 0, []
+        self.other = 1 - lax.axis_index(CORE)
+
+    def leaving(self, like):
+        self.leave.append(like)
+        return len(self.leave) - 1
+
+    def landing(self):
+        self.arrivals += 1
+        return self.arrivals - 1
 
     def copy(self, source, target, to, send_at, recv_at):
         return pltpu.make_async_remote_copy(
@@ -35,25 +40,26 @@
             device_id_type=MESH_ID,
         )
 
-    def send(self, source, target, to, recv_at):
-        copy = self.copy(source, target, to, self.sent, recv_at)
-        self.sent += 1
-        copy.start()
-        self.last.append(copy)
-
-    def arrived(self, like, to, recv_at):
-        self.copy(like, like, to, 0, recv_at).wait_recv()
+    def send(self, source, target, to, send_at, recv_at):
+        self.copy(source, target, to, send_at, recv_at).start()
+
+    def landed(self, like, recv_at):
+        self.copy(like, like, {CORE: self.other}, 0, recv_at).wait_recv()
 
     def drain(self):
-        for copy in self.last:
-            copy.wait_send()
+        for at, like in enumerate(self.leave):
+            self.copy(like, like, {CORE: self.other}, at, 0).wait_send()
 
 
 def greet(peers):
-    barrier = pltpu.get_barrier_semaphore()
     for peer in peers:
-        pl.semaphore_signal(barrier, inc=1, device_id=peer, device_id_type=MESH_ID)
-    pl.semaphore_wait(barrier, len(peers))
+        pl.semaphore_signal(
+            pltpu.get_barrier_semaphore(), inc=1, device_id=peer, device_id_type=MESH_ID
+        )
+
+
+def greeted(peers):
+    pl.semaphore_wait(pltpu.get_barrier_semaphore(), len(peers))
 
 
 def ring_places(axis):
@@ -78,7 +84,9 @@
         self.core = lax.axis_index(CORE)
         self.rings = [ring_places(axis) for axis in RINGS]
         self.chunks = range(refs[0].shape[0])
-        self.running = [None] * len(self.chunks)
+        self.leave = [wires.leaving(ref.at[:, pl.ds(0, 3)]) for ref in refs[:3]]
+        self.leave.append(wires.leaving(refs[2].at[:, 0, :, :, 0]))
+        self.land = [[wires.landing() for _ in self.chunks] for _ in range(4)]
 
     def spot(self, chunk, dim, index, core_at=slice(None)):
         at = [chunk, slice(None), slice(None), slice(None), core_at]
@@ -91,52 +99,45 @@
         source, target = self.refs[phase], self.refs[phase + 1]
         axis = RINGS[dim]
         me, up, down, across = self.rings[dim]
+        leave, land = self.leave[phase], self.land[phase][chunk]
         if phase < 2:
-            base = wires.slots(3)
-            for way, to in enumerate((across, up, down)):
+            for to in (across, up, down):
                 wires.send(
                     source.at[self.spot(chunk, dim, to)],
                     target.at[self.spot(chunk, dim, me)],
                     {axis: to},
-                    base + way,
+                    leave,
+                    land,
                 )
             own = self.spot(chunk, dim, me)
         else:
-            base = wires.slots(7)
-            for way, to in enumerate((across, up, down)):
+            own = self.spot(chunk, dim, me, core)
+            for to in (across, up, down):
                 for core_at in (0, 1):
                     wires.send(
                         source.at[self.spot(chunk, dim, to, core_at)],
-                        target.at[self.spot(chunk, dim, me, core)],
+                        target.at[own],
                         {axis: to, CORE: core_at},
-                        base + 2 * way + core,
+                        leave,
+                        land,
                     )
             wires.send(
                 source.at[self.spot(chunk, dim, me, other)],
-                target.at[self.spot(chunk, dim, me, core)],
+                target.at[own],
                 {CORE: other},
-                base + 6,
+                self.leave[3],
+                self.land[3][chunk],
             )
-            own = self.spot(chunk, dim, me, core)
         target[own] = source[own]
-        self.running[chunk] = base
 
     def finish(self, phase, chunk):
-        dim = (chunk + phase) % 3
-        me, up, _, _ = self.rings[dim]
-        if phase < 2:
-            like, number = self.refs[phase + 1].at[self.spot(chunk, dim, me)], 3
-        else:
-            like, number = self.refs[phase + 1].at[self.spot(chunk, dim, me, self.core)], 7
-        for at in range(number):
-            self.wires.arrived(like, {RINGS[dim]: up}, self.running[chunk] + at)
-
-    def begin(self):
-        for chunk in self.chunks:
-            self.start(0, chunk)
-
-    def advance(self, phase):
-        for chunk in self.chunks:
+        target = self.refs[phase + 1]
+        self.wires.landed(target.at[chunk, pl.ds(0, 3)], self.land[phase][chunk])
+        if phase == 2:
+            self.wires.landed(target.at[chunk, 0, :, :, 0], self.land[3][chunk])
+
+    def advance(self, phase, chunks=None):
+        for chunk in self.chunks if chunks is None else chunks:
             self.finish(phase, chunk)
             if phase < 2:
                 self.start(phase + 1, chunk)
@@ -147,16 +148,16 @@
         self.wires = wires
         self.me = lax.axis_index("member_0") * 2 + lax.axis_index(CORE)
 
-    def start(self, source_of, target):
-        self.base = self.wires.slots(7)
+    def start(self, source_of, targets):
+        self.like = targets.at[pl.ds(0, 7)]
+        leave, self.land = self.wires.leaving(self.like), self.wires.landing()
         for step in range(1, 8):
             to = lax.rem(self.me + step, 8)
             where = {"member_0": to // 2, CORE: lax.rem(to, 2)}
-            self.wires.send(source_of(to), target, where, self.base + step - 1)
-
-    def finish(self, like):
-        for step in range(7):
-            self.wires.arrived(like, {CORE: 1 - lax.axis_index(CORE)}, self.base + step)
+            self.wires.send(source_of(to), targets.at[self.me], where, leave, self.land)
+
+    def finish(self):
+        self.wires.landed(self.like, self.land)
 
 
 class Ring:
@@ -167,20 +168,22 @@
     def order(self):
         return (self.across, self.up, self.down)
 
-    def open(self):
-        self.base = self.wires.slots(3)
-
-    def send(self, way, source, target):
-        self.wires.send(source, target, {self.axis: self.order()[way]}, self.base + way)
-
-    def start(self, source_of, target):
-        self.open()
+    def open(self, targets):
+        self.like, self.target = targets.at[pl.ds(0, 3)], targets.at[self.me]
+        self.leave, self.land = self.wires.leaving(self.like), self.wires.landing()
+
+    def send(self, way, source):
+        self.wires.send(
+            source, self.target, {self.axis: self.order()[way]}, self.leave, self.land
+        )
+
+    def start(self, source_of, targets):
+        self.open(targets)
         for way, to in enumerate(self.order()):
-            self.send(way, source_of(to), target)
-
-    def finish(self, like):
-        for way in range(3):
-            self.wires.arrived(like, {self.axis: self.up}, self.base + way)
+            self.send(way, source_of(to))
+
+    def finish(self):
+        self.wires.landed(self.like, self.land)
 
 
 def diagonal(rows, lanes):
@@ -196,14 +199,14 @@
 
 
 def step_kernel(
-    samples_ref,
-    cell_ref,
-    fine_ref,
+    samples_in,
+    cell_in,
+    fine_in,
     sharp_ref,
-    mid_ref,
-    mids_ref,
-    route_ref,
-    coarse_ref,
+    mid_in,
+    mids_in,
+    route_in,
+    coarse_in,
     fine_new_ref,
     mids_new_ref,
     coarse_new_ref,
@@ -243,10 +246,35 @@
     second_sum,
     third_sum,
     total,
+    samples_ref,
+    cell_ref,
+    fine_ref,
+    mid_ref,
+    mids_ref,
+    route_ref,
+    coarse_ref,
+    route_wide,
+    load_sem,
     send_sem,
     recv_sem,
 ):
     f32, bf16 = jnp.float32, jnp.bfloat16
+    loads = [
+        pltpu.make_async_copy(source, target, load_sem.at[at])
+        for at, (source, target) in enumerate(
+            (
+                (cell_in, cell_ref),
+                (samples_in, samples_ref),
+                (route_in, route_ref),
+                (fine_in, fine_ref),
+                (mid_in, mid_ref),
+                (mids_in, mids_ref),
+                (coarse_in, coarse_ref),
+            )
+        )
+    ]
+    for load in loads:
+        load.start()
     wires = Wires(send_sem, recv_sem)
     core = lax.axis_index(CORE)
     other = 1 - core
@@ -260,6 +288,9 @@
     mid_dev = mids_ref.shape[0]
     split = half_a.shape[-1]
 
+    peers = ring_peers(True)
+    greet(peers)
+    loads[0].wait()
     cell_row = cell_ref[...]
     cell_column = as_column(cell_row, row_count)
     earlier = lax.broadcasted_iota(jnp.int32, (row_count, row_count), 0) < lax.broadcasted_iota(
@@ -273,29 +304,34 @@
     picked = jnp.where(place == slot_row, 1.0, 0.0).astype(bf16)
     used = jnp.dot(picked, jnp.ones((row_count, lanes), bf16), preferred_element_type=f32) > 0.5
 
-    greet(ring_peers(True))
+    for load in loads[1:]:
+        load.wait()
+    route_wide[...] = jnp.zeros_like(route_wide)
+    route_wide[:, pl.ds(0, mid_dev)] = route_ref[...]
+    greeted(peers)
     moving = Exchange(wires, (outgoing, there_a, there_b, arrived))
-    for chunk in range(chunks):
+    for chunk in range(0, chunks, 2):
         lines = jnp.dot(
-            picked, samples_ref[:, pl.ds(chunk * lanes, lanes)], preferred_element_type=f32
-        )
-        lines = jnp.where(used, lines, EMPTY)
-        outgoing[chunk] = lines.reshape(outgoing.shape[1:]).astype(bf16)
-        moving.start(0, chunk)
+            picked, samples_ref[:, pl.ds(chunk * lanes, 2 * lanes)], preferred_element_type=f32
+        )
+        for at in range(2):
+            line = jnp.where(used, lines[:, at * lanes : (at + 1) * lanes], EMPTY)
+            outgoing[chunk + at] = line.reshape(outgoing.shape[1:]).astype(bf16)
+            moving.start(0, chunk + at)
     octet = Octet(wires)
     xs, zs, ys = Ring(wires, "member_0"), Ring(wires, "member_1"), Ring(wires, "group")
     maps_ring = Ring(wires, "member_1")
-    octet.start(lambda to: route_ref, maps.at[zs.me, octet.me])
-    maps[zs.me, octet.me] = route_ref[...]
+    octet.start(lambda to: route_wide, maps.at[zs.me])
+    maps[zs.me, octet.me] = route_wide[...]
     slot_column = as_column(slot_row, row_count)
     along = lax.broadcasted_iota(jnp.int32, (row_count, slots), 1)
     chosen[...] = jnp.where(along == slot_column, 1.0, 0.0).astype(bf16)
-    octet.finish(maps.at[zs.me, octet.me])
-    maps_ring.start(lambda to: maps.at[zs.me], maps.at[zs.me])
     moving.advance(0)
-    maps_ring.finish(maps.at[zs.me])
+    octet.finish()
+    maps_ring.start(lambda to: maps.at[zs.me], maps)
     moving.advance(1)
     moving.advance(2)
+    maps_ring.finish()
 
     for chunk in range(chunks):
         piece = arrived[chunk].astype(f32).reshape(slots, lanes)
@@ -367,24 +403,26 @@
         )
 
     order_x = xs.order() + (xs.me,)
-    swap, swap_m = wires.slots(4), wires.slots(4)
+    swap = [wires.landing() for _ in range(4)]
+    swap_m = [wires.landing() for _ in range(4)]
+    leave, leave_m = wires.leaving(give), wires.leaving(give_m)
     for way, x in enumerate(order_x):
         part = mid_part(x, other)
         for z in range(4):
             give[x, z] = part[z * mid_dev : (z + 1) * mid_dev, :width].astype(bf16)
             give_m[x, z] = mass_row(part, z)
-        wires.send(give.at[x], core_in.at[x], {CORE: other}, swap + way)
-        wires.send(give_m.at[x], core_m.at[x], {CORE: other}, swap_m + way)
+        wires.send(give.at[x], core_in.at[x], {CORE: other}, leave, swap[way])
+        wires.send(give_m.at[x], core_m.at[x], {CORE: other}, leave_m, swap_m[way])
     xs_m = Ring(wires, "member_0")
-    xs.open()
-    xs_m.open()
+    xs.open(near_a)
+    xs_m.open(near_m)
     level = lax.broadcasted_iota(jnp.int32, (coarse_ref.shape[0], lanes), 0)
     coarse_part = jnp.zeros((coarse_ref.shape[0], width), f32)
     coarse_mass = jnp.zeros((coarse_ref.shape[0], lanes), f32)
     for way, x in enumerate(order_x):
         part = mid_part(x, core)
-        wires.arrived(core_in.at[x], {CORE: other}, swap + way)
-        wires.arrived(core_m.at[x], {CORE: other}, swap_m + way)
+        wires.landed(core_in.at[x], swap[way])
+        wires.landed(core_m.at[x], swap_m[way])
         for z in range(4):
             half = part[z * mid_dev : (z + 1) * mid_dev, :width] + core_in[x, z].astype(f32)
             half = half.astype(bf16)
@@ -400,53 +438,64 @@
                 preferred_element_type=f32,
             )
         if way < 3:
-            xs.send(way, half_a.at[x], near_a.at[xs.me])
-            xs_m.send(way, half_m.at[x], near_m.at[xs.me])
-    zs.start(lambda to: half_b.at[to], near_b.at[zs.me])
+            xs.send(way, half_a.at[x])
+            xs_m.send(way, half_m.at[x])
+    zs.start(lambda to: half_b.at[to], near_b)
     coarse_mass = jnp.broadcast_to(jnp.sum(coarse_mass, axis=1, keepdims=True), coarse_mass.shape)
     for at in range(8):
-        part_c[at, :, pl.ds(0, width)] = coarse_part[8 * at : 8 * at + 8]
-        part_c[at, :, pl.ds(width, lanes)] = coarse_mass[8 * at : 8 * at + 8]
-    octet.start(lambda to: part_c.at[to], first_sum.at[octet.me])
+        part_c[at, :, pl.ds(0, width)] = coarse_part[8 * at : 8 * at + 8].astype(bf16)
+        part_c[at, :, pl.ds(width, lanes)] = coarse_mass[8 * at : 8 * at + 8].astype(bf16)
+    octet.start(lambda to: part_c.at[to], first_sum)
     first_sum[octet.me] = part_c[octet.me]
 
     homing.advance(0)
-
-    octet.finish(first_sum.at[octet.me])
-    second_sum[zs.me] = sum(first_sum[at] for at in range(8))
+    homing.advance(1, (2, 5))
+
+    xs.finish()
+    xs_m.finish()
+    octet.finish()
+    second_sum[zs.me] = sum(first_sum[at].astype(f32) for at in range(8))
     zs_coarse = Ring(wires, "member_1")
-    zs_coarse.start(lambda to: second_sum.at[zs.me], second_sum.at[zs.me])
-
-    xs.finish(near_a.at[xs.me])
-    xs_m.finish(near_m.at[xs.me])
+    zs_coarse.start(lambda to: second_sum.at[zs.me], second_sum)
     for z in range(4):
         line_a[z] = (
             half_a[xs.me, z].astype(f32) + sum(near_a[at, z].astype(f32) for at in xs.order())
         ).astype(bf16)
         line_m[z] = half_m[xs.me, z] + sum(near_m[at, z] for at in xs.order())
     zs_late, zs_m, xs_late = Ring(wires, "member_1"), Ring(wires, "member_1"), Ring(wires, "member_0")
-    zs_late.start(lambda to: line_a.at[to], far_a.at[zs.me])
-    zs_m.start(lambda to: line_m.at[to], far_m.at[zs.me])
-    zs.finish(near_b.at[zs.me])
+    zs_late.start(lambda to: line_a.at[to], far_a)
+    zs_m.start(lambda to: line_m.at[to], far_m)
+    zs.finish()
     for x in range(4):
         line_b[x] = (
             half_b[zs.me, x].astype(f32) + sum(near_b[at, x].astype(f32) for at in zs.order())
         ).astype(bf16)
-    xs_late.start(lambda to: line_b.at[to], far_b.at[xs.me])
-
-    zs_coarse.finish(second_sum.at[zs.me])
+    xs_late.start(lambda to: line_b.at[to], far_b)
+
+    homing.advance(1, (0, 3))
+    zs_coarse.finish()
     third_sum[ys.me] = sum(second_sum[at] for at in range(4))
-    ys.start(lambda to: third_sum.at[ys.me], third_sum.at[ys.me])
-
-    homing.advance(1)
-
-    ys.finish(third_sum.at[ys.me])
-    total[octet.me] = sum(third_sum[at] for at in range(4))
-    octet.start(lambda to: total.at[octet.me], total.at[octet.me])
-
-    zs_late.finish(far_a.at[zs.me])
-    zs_m.finish(far_m.at[zs.me])
-    xs_late.finish(far_b.at[xs.me])
+    ys.start(lambda to: third_sum.at[ys.me], third_sum)
+    homing.advance(1, (1, 4))
+
+    ys.finish()
+    total[octet.me] = sum(third_sum[at] for at in range(4)).astype(bf16)
+    octet.start(lambda to: total.at[octet.me], total)
+
+    def reconstruct(pair):
+        homing.advance(2, pair)
+        lines = jnp.concatenate(
+            [returned[chunk].astype(f32).reshape(slots, lanes).astype(bf16) for chunk in pair],
+            axis=1,
+        )
+        lines = jnp.dot(chosen[...], lines, preferred_element_type=f32).astype(bf16)
+        for at, chunk in enumerate(pair):
+            rec_ref[:, pl.ds(chunk * lanes, lanes)] = lines[:, at * lanes : (at + 1) * lanes]
+
+    reconstruct((2, 5))
+    zs_late.finish()
+    zs_m.finish()
+    xs_late.finish()
     masses = line_m[zs.me] + sum(far_m[at] for at in zs.order())
     share = 1.0 / (as_column(masses, mid_dev) + 1.0)
     own_a = line_a[zs.me].astype(f32) + sum(far_a[at].astype(f32) for at in zs.order())
@@ -454,19 +503,18 @@
     mids_new_ref[:, pl.ds(0, split)] = (own_a + mids_ref[:, pl.ds(0, split)]) * share
     mids_new_ref[:, pl.ds(split, split)] = (own_b + mids_ref[:, pl.ds(split, split)]) * share
 
-    octet.finish(total.at[octet.me])
+    reconstruct((0, 3))
+    reconstruct((1, 4))
+
+    octet.finish()
     for at in range(8):
         here = pl.ds(8 * at, 8)
-        share = 1.0 / (total[at, :, pl.ds(width, lanes)] + 1.0)
+        share = 1.0 / (total[at, :, pl.ds(width, lanes)].astype(f32) + 1.0)
         for chunk in range(chunks):
             there = pl.ds(chunk * lanes, lanes)
-            coarse_new_ref[here, there] = (total[at, :, there] + coarse_ref[here, there]) * share
-    for chunk in range(chunks):
-        homing.finish(2, chunk)
-        lines = returned[chunk].astype(f32).reshape(slots, lanes).astype(bf16)
-        rec_ref[:, pl.ds(chunk * lanes, lanes)] = jnp.dot(
-            chosen[...], lines, preferred_element_type=f32
-        ).astype(bf16)
+            coarse_new_ref[here, there] = (
+                total[at, :, there].astype(f32) + coarse_ref[here, there]
+            ) * share
     wires.drain()
 
 
@@ -492,18 +540,19 @@
     split = width // 2
     moved = (chunks, 4, 4, 4, 2, 2 * cells, lanes)
     eighth = (coarse_total // 8, width + lanes)
-    copies = 2 * 13 * chunks + 3 * 7 + 9 * 3 + 8
+    leaves, lands = 2 * 4 + 3 + 9 + 2, 2 * 4 * chunks + 3 + 9 + 8
     f32, bf16 = jnp.float32, jnp.bfloat16
     vmem = pl.BlockSpec(memory_space=pltpu.VMEM)
-    return pl.pallas_call(
+    hbm = pl.BlockSpec(memory_space=pltpu.HBM)
+    results = pl.pallas_call(
         step_kernel,
         out_shape=(
-            jax.ShapeDtypeStruct((fine_total, width), f32),
-            jax.ShapeDtypeStruct((mid_dev, width), f32),
-            jax.ShapeDtypeStruct((coarse_total, width), f32),
-            jax.ShapeDtypeStruct((row_count, width), bf16),
+            pltpu.VMEM((fine_total, width), f32),
+            pltpu.VMEM((mid_dev, width), f32),
+            pltpu.VMEM((coarse_total, width), f32),
+            pltpu.VMEM((row_count, width), bf16),
         ),
-        in_specs=[vmem, vmem, vmem, pl.BlockSpec(memory_space=pltpu.SMEM)] + [vmem] * 4,
+        in_specs=[hbm] * 3 + [pl.BlockSpec(memory_space=pltpu.SMEM)] + [hbm] * 4,
         out_specs=(vmem,) * 4,
         scratch_shapes=[pltpu.VMEM(moved, bf16)] * 8
         + [
@@ -520,15 +569,24 @@
         + [pltpu.VMEM((4, mid_dev, split), bf16)] * 4
         + [pltpu.VMEM((4, 4, 1, lanes), f32)] * 4
         + [pltpu.VMEM((4, 1, lanes), f32)] * 2
-        + [pltpu.VMEM((8,) + eighth, f32)] * 2
+        + [pltpu.VMEM((8,) + eighth, bf16)] * 2
         + [pltpu.VMEM((4,) + eighth, f32)] * 2
         + [
-            pltpu.VMEM((8,) + eighth, f32),
-            pltpu.SemaphoreType.DMA((copies,)),
-            pltpu.SemaphoreType.DMA((copies,)),
+            pltpu.VMEM((8,) + eighth, bf16),
+            pltpu.VMEM((row_count, width), bf16),
+            pltpu.VMEM((1, row_count), jnp.int32),
+            pltpu.VMEM((fine_total, width), bf16),
+            pltpu.VMEM((1, fine_total), jnp.int32),
+            pltpu.VMEM((mid_dev, width), f32),
+            pltpu.VMEM((1, mid_dev), jnp.int32),
+            pltpu.VMEM((coarse_total, width), f32),
+            pltpu.VMEM((1, lanes), jnp.int32),
+            pltpu.SemaphoreType.DMA((7,)),
+            pltpu.SemaphoreType.DMA((leaves,)),
+            pltpu.SemaphoreType.DMA((lands,)),
         ],
         compiler_params=pltpu.CompilerParams(
-            collective_id=0, has_side_effects=True, vmem_limit_bytes=60 * 1024 * 1024
+            collective_id=0, has_side_effects=True, vmem_limit_bytes=54 * 1024 * 1024
         ),
         name="lloyd_step",
     )(
@@ -538,9 +596,29 @@
         sharpness,
         mid_of_fine.reshape(1, fine_total),
         mid_centroids,
-        jnp.pad(coarse_of_mid, (0, lanes - mid_dev))[None],
+        coarse_of_mid.reshape(1, mid_dev),
         coarse_centroids,
     )
+    return pl.pallas_call(
+        put_out_kernel,
+        out_shape=tuple(jax.ShapeDtypeStruct(one.shape, one.dtype) for one in results),
+        in_specs=[vmem] * 4,
+        out_specs=(hbm,) * 4,
+        scratch_shapes=[pltpu.SemaphoreType.DMA((4,))],
+        compiler_params=pltpu.CompilerParams(vmem_limit_bytes=1024 * 1024),
+        name="put_out",
+    )(*results)
+
+
+def put_out_kernel(*refs):
+    copies = [
+        pltpu.make_async_copy(source, target, refs[8].at[at])
+        for at, (source, target) in enumerate(zip(refs[:4], refs[4:8]))
+    ]
+    for copy in copies:
+        copy.start()
+    for copy in copies:
+        copy.wait()
 
 
 def solution(mesh):

time: 92.3 us -> 71.8 us (0.78)
  Pallas kernels: 84.2 us -> 70.9 us
  local copies, waits for them, and re-layouts: 7.26 us -> 0 us
    pallas_call x1 -> x2, Pallas kernels: 84.2 us -> 70.9 us  [the longest x1 68.8 us: shards(): pl.pallas_call(step_kernel, out_shape=(pltpu.VMEM((fine_total, width), f3...]
    unnamed x10 -> x0, local copies, waits for them, and re-layouts: 6.1 us -> none
    broadcast_in_dim x1 -> x0, local copies, waits for them, and re-layouts: 1.17 us -> none  [shards(): jnp.pad(coarse_of_mid, (0, lanes - mid_dev))[None]]
where the time goes in v4:
time: 71.8 us; the launch traced here: 71.7 us
  Pallas kernels  70.9 us (99%)
  between operations  0.8 us (1%)
    pallas_call x1, Pallas kernels, shards(): pl.pallas_call(step_kernel, out_shape=(pltpu.VMEM((fine_total, width), f3...  68.8 us
    pallas_call x1, Pallas kernels, shards(): pl.pallas_call(put_out_kernel, out_shape=tuple((jax.ShapeDtypeStruct(one....  2.08 us

profile of v4, /device:TPU:1, one launch (start us, length us, event | category | flops | bytes accessed | tf_op | source)
XLA Modules:
  0.0 71.7 jit_solution(12701349681285131423)
XLA Ops:
  0.6 68.8 %lloyd_step.1 = (f32[1024,768]{1,0:T(8,128)S(1)}, f32[64,768]{1,0:T(8,128)S(1)}, f32[64,768]{1,0:T(8,128)S(1)}, bf16[512,768]{1,0:T(8,128)(2,1)S(1)}) custom-call(bf16[512,768]{1,0:T(8,128)(2,1)} %samples_in.1, s32[1,512]{1,0:T(1,128)} %bitcast.4, bf16[1024,768]{1,0:T(8,128)(2,1)} %fine_in.1, f32[4]{0:T(128)} %sharp_ref.1, s32[1,1024]{1,0:T(1,128)} %bitcast.3, ...), custom_call_target="tpu_custom_call" | custom-call | tf_op jit(solution)/shard_map/lloyd_step/pallas_call | solution.py:547
  69.4 2.1 %put_out.1 = (f32[1024,768]{1,0:T(8,128)}, f32[64,768]{1,0:T(8,128)}, f32[64,768]{1,0:T(8,128)}, bf16[512,768]{1,0:T(8,128)(2,1)}) custom-call(f32[1024,768]{1,0:T(8,128)S(1)} %get-tuple-element.8.refs_0_, f32[64,768]{1,0:T(8,128)S(1)} %get-tuple-element.9.refs_1_, f32[64,768]{1,0:T(8,128)S(1)} %get-tuple-element.10.refs_2_, ...), custom_call_target="tpu_custom_call" | custom-call | tf_op jit(solution)/shard_map/put_out/pallas_call | solution.py:602

commit v5 on v4

--- a/solution.py
+++ b/solution.py
@@ -186,6 +186,51 @@
         self.wires.landed(self.like, self.land)
 
 
+class Halves:
+    def __init__(self, wires, ring, relay, near):
+        self.wires, self.ring, self.relay, self.near = wires, ring, relay, near
+        self.leave_relay, self.leave_near = wires.leaving(relay), wires.leaving(near)
+        self.land_relay = [wires.landing() for _ in range(2)]
+        self.land_near = wires.landing()
+
+    def send_near(self, blocks, way, half):
+        to = (self.ring.up, self.ring.down)[way]
+        part = pl.ds(2 * half, 2)
+        self.wires.send(
+            blocks.at[to, part],
+            self.near.at[way, part],
+            {self.ring.axis: to},
+            self.leave_near,
+            self.land_near,
+        )
+
+    def offer(self, step, blocks):
+        if step > 0:
+            self.send_near(blocks, step - 1, 2 - step)
+            return
+        for way, to in enumerate((self.ring.up, self.ring.down)):
+            self.wires.send(
+                blocks.at[self.ring.across, pl.ds(2 * way, 2)],
+                self.relay.at[way],
+                {self.ring.axis: to},
+                self.leave_relay,
+                self.land_relay[way],
+            )
+
+    def pass_on(self, blocks):
+        for way, to in enumerate((self.ring.up, self.ring.down)):
+            self.wires.landed(self.relay.at[way], self.land_relay[way])
+            for at in range(2):
+                blocks[to, 2 * way + at] = (
+                    blocks[to, 2 * way + at].astype(jnp.float32)
+                    + self.relay[way, at].astype(jnp.float32)
+                ).astype(jnp.bfloat16)
+            self.send_near(blocks, way, way)
+
+    def finish(self):
+        self.wires.landed(self.near, self.land_near)
+
+
 def diagonal(rows, lanes):
     return lax.broadcasted_iota(jnp.int32, (rows, lanes), 0) == lax.broadcasted_iota(
         jnp.int32, (rows, lanes), 1
@@ -221,6 +266,11 @@
     returned,
     wide,
     back,
+    lines,
+    products,
+    norms,
+    shares,
+    turned,
     resps,
     sums,
     chosen,
@@ -231,6 +281,8 @@
     half_b,
     near_a,
     near_b,
+    relay_a,
+    relay_b,
     line_a,
     line_b,
     far_a,
@@ -311,11 +363,11 @@
     greeted(peers)
     moving = Exchange(wires, (outgoing, there_a, there_b, arrived))
     for chunk in range(0, chunks, 2):
-        lines = jnp.dot(
+        put = jnp.dot(
             picked, samples_ref[:, pl.ds(chunk * lanes, 2 * lanes)], preferred_element_type=f32
         )
         for at in range(2):
-            line = jnp.where(used, lines[:, at * lanes : (at + 1) * lanes], EMPTY)
+            line = jnp.where(used, put[:, at * lanes : (at + 1) * lanes], EMPTY)
             outgoing[chunk + at] = line.reshape(outgoing.shape[1:]).astype(bf16)
             moving.start(0, chunk + at)
     octet = Octet(wires)
@@ -329,62 +381,68 @@
     moving.advance(0)
     octet.finish()
     maps_ring.start(lambda to: maps.at[zs.me], maps)
-    moving.advance(1)
-    moving.advance(2)
-    maps_ring.finish()
-
-    for chunk in range(chunks):
-        piece = arrived[chunk].astype(f32).reshape(slots, lanes)
-        wide[chunk] = jnp.where(piece > 0.5 * EMPTY, 0.0, piece)
-        if chunk == 0:
-            wide[chunks] = jnp.where(piece > 0.5 * EMPTY, 0.0, 1.0)
-
-    def cell_rows(cell, number):
-        spots = [pl.ds(cell * 2 + most, sources, stride=per_source) for most in range(2)]
-        return jnp.concatenate(
-            [
-                jnp.concatenate([wide[chunk, at, :] for at in spots], axis=0).astype(bf16)
-                for chunk in range(number)
-            ],
-            axis=1,
-        )
-
-    for cell in range(cells):
-        centres = fine_ref[pl.ds(cell * fine, fine), :]
-        centres_wide = centres.astype(f32)
-        norms = jnp.sum(centres_wide * centres_wide, axis=1, keepdims=True)
-        products = lax.dot_general(
-            centres,
-            cell_rows(cell, chunks),
-            (((1,), (1,)), ((), ())),
-            preferred_element_type=f32,
-        )
-        scores = (products - 0.5 * norms) * (sharp_ref[cell] / math.sqrt(width))
-        exponent = jnp.exp(scores - jnp.max(scores, axis=0, keepdims=True))
-        resp = (exponent / jnp.sum(exponent, axis=0, keepdims=True)).astype(bf16)
-        resps[cell] = resp
-        lines = lax.dot_general(resp, centres, (((0,), (0,)), ((), ())), preferred_element_type=f32)
-        for chunk in range(chunks):
-            for most in range(2):
-                back[chunk, pl.ds(cell * 2 + most, sources, stride=per_source), :] = lines[
-                    most * sources : (most + 1) * sources, chunk * lanes : (chunk + 1) * lanes
-                ]
-    homing = Exchange(wires, (rebuilt, back_a, back_b, returned))
-    for chunk in range(chunks):
-        rebuilt[chunk] = back[chunk].reshape(rebuilt.shape[1:]).astype(bf16)
-        homing.start(0, chunk)
-
     for cell in range(cells):
         here = pl.ds(cell * fine, fine)
-        weighted = jnp.dot(resps[cell], cell_rows(cell, chunks + 1), preferred_element_type=f32)
+        centres_wide = fine_ref[here, :].astype(f32)
+        norms[here, :] = jnp.broadcast_to(
+            jnp.sum(centres_wide * centres_wide, axis=1, keepdims=True), (fine, lanes)
+        )
+    moving.advance(1)
+    maps_ring.finish()
+
+    for pair in range(0, chunks, 2):
+        moving.advance(2, (pair, pair + 1))
+        for chunk in (pair, pair + 1):
+            piece = arrived[chunk].astype(f32).reshape(slots, lanes)
+            wide[chunk] = jnp.where(piece > 0.5 * EMPTY, 0.0, piece)
+            if chunk == 0:
+                wide[chunks] = jnp.where(piece > 0.5 * EMPTY, 0.0, 1.0)
+        at = pl.ds(pair * lanes, 2 * lanes)
+        for cell in range(cells):
+            spots = [pl.ds(cell * 2 + most, sources, stride=per_source) for most in range(2)]
+            for chunk in (pair, pair + 1) + ((chunks,) if pair == 0 else ()):
+                lines[cell, :, pl.ds(chunk * lanes, lanes)] = jnp.concatenate(
+                    [wide[chunk, spot, :] for spot in spots], axis=0
+                ).astype(bf16)
+            product = lax.dot_general(
+                fine_ref[pl.ds(cell * fine, fine), at],
+                lines[cell, :, at],
+                (((1,), (1,)), ((), ())),
+                preferred_element_type=f32,
+            )
+            products[cell] = product if pair == 0 else products[cell] + product
+
+    for cell in range(cells):
+        half_norms = 0.5 * norms[pl.ds(cell * fine, fine), :]
+        half_norms = jnp.concatenate([half_norms, half_norms], axis=1)
+        scores = (products[cell] - half_norms) * (sharp_ref[cell] / math.sqrt(width))
+        exponent = jnp.exp(scores - jnp.max(scores, axis=0, keepdims=True))
+        resp = exponent / jnp.sum(exponent, axis=0, keepdims=True)
+        resps[cell] = resp.astype(bf16)
+        turned[cell] = resp.T.astype(bf16)
+    homing = Exchange(wires, (rebuilt, back_a, back_b, returned))
+    for pair in range(0, chunks, 2):
+        for cell in range(cells):
+            row = jnp.dot(
+                turned[cell],
+                fine_ref[pl.ds(cell * fine, fine), pl.ds(pair * lanes, 2 * lanes)],
+                preferred_element_type=f32,
+            )
+            for at in range(2):
+                for most in range(2):
+                    back[pair + at, pl.ds(cell * 2 + most, sources, stride=per_source), :] = row[
+                        most * sources : (most + 1) * sources, at * lanes : (at + 1) * lanes
+                    ]
+        for chunk in (pair, pair + 1):
+            rebuilt[chunk] = back[chunk].reshape(rebuilt.shape[1:]).astype(bf16)
+            homing.start(0, chunk)
+
+    for cell in range(cells):
+        here = pl.ds(cell * fine, fine)
+        weighted = jnp.dot(resps[cell], lines[cell], preferred_element_type=f32)
         sums[here, :] = weighted.astype(bf16)
-        centres_wide = fine_ref[here, :].astype(f32)
-        share = 1.0 / (weighted[:, width:] + 1.0)
-        for chunk in range(chunks):
-            at = slice(chunk * lanes, (chunk + 1) * lanes)
-            fine_new_ref[here, pl.ds(chunk * lanes, lanes)] = (
-                weighted[:, at] + centres_wide[:, at]
-            ) * share
+        fine_new_ref[here, :] = weighted[:, :width]
+        shares[here, :] = 1.0 / (weighted[:, width:] + 1.0)
 
     rows_of = 4 * mid_dev
     local_mid = mid_ref[...] - lax.axis_index("group") * (32 * mid_dev)
@@ -414,8 +472,8 @@
         wires.send(give.at[x], core_in.at[x], {CORE: other}, leave, swap[way])
         wires.send(give_m.at[x], core_m.at[x], {CORE: other}, leave_m, swap_m[way])
     xs_m = Ring(wires, "member_0")
-    xs.open(near_a)
     xs_m.open(near_m)
+    ring_a, ring_b = Halves(wires, xs, relay_a, near_a), Halves(wires, zs, relay_b, near_b)
     level = lax.broadcasted_iota(jnp.int32, (coarse_ref.shape[0], lanes), 0)
     coarse_part = jnp.zeros((coarse_ref.shape[0], width), f32)
     coarse_mass = jnp.zeros((coarse_ref.shape[0], lanes), f32)
@@ -438,9 +496,11 @@
                 preferred_element_type=f32,
             )
         if way < 3:
-            xs.send(way, half_a.at[x])
+            ring_a.offer(way, half_a)
             xs_m.send(way, half_m.at[x])
-    zs.start(lambda to: half_b.at[to], near_b)
+    ring_a.pass_on(half_a)
+    for way in range(3):
+        ring_b.offer(way, half_b)
     coarse_mass = jnp.broadcast_to(jnp.sum(coarse_mass, axis=1, keepdims=True), coarse_mass.shape)
     for at in range(8):
         part_c[at, :, pl.ds(0, width)] = coarse_part[8 * at : 8 * at + 8].astype(bf16)
@@ -448,49 +508,57 @@
     octet.start(lambda to: part_c.at[to], first_sum)
     first_sum[octet.me] = part_c[octet.me]
 
-    homing.advance(0)
-    homing.advance(1, (2, 5))
-
-    xs.finish()
+    homing.advance(0, (2, 5, 0, 3))
+    ring_b.pass_on(half_b)
+    homing.advance(0, (1, 4))
+    for cell in range(cells):
+        here = pl.ds(cell * fine, fine)
+        for chunk in range(chunks):
+            at = pl.ds(chunk * lanes, lanes)
+            fine_new_ref[here, at] = (
+                fine_new_ref[here, at] + fine_ref[here, at].astype(f32)
+            ) * shares[here, :]
+    ring_a.finish()
     xs_m.finish()
     octet.finish()
-    second_sum[zs.me] = sum(first_sum[at].astype(f32) for at in range(8))
-    zs_coarse = Ring(wires, "member_1")
-    zs_coarse.start(lambda to: second_sum.at[zs.me], second_sum)
+    second_sum[ys.me] = sum(first_sum[at].astype(f32) for at in range(8))
+    ys.start(lambda to: second_sum.at[ys.me], second_sum)
     for z in range(4):
         line_a[z] = (
-            half_a[xs.me, z].astype(f32) + sum(near_a[at, z].astype(f32) for at in xs.order())
+            half_a[xs.me, z].astype(f32) + near_a[0, z].astype(f32) + near_a[1, z].astype(f32)
         ).astype(bf16)
         line_m[z] = half_m[xs.me, z] + sum(near_m[at, z] for at in xs.order())
     zs_late, zs_m, xs_late = Ring(wires, "member_1"), Ring(wires, "member_1"), Ring(wires, "member_0")
     zs_late.start(lambda to: line_a.at[to], far_a)
     zs_m.start(lambda to: line_m.at[to], far_m)
-    zs.finish()
+
+    homing.advance(1, (2, 5))
+    ys.finish()
+    third_sum[zs.me] = sum(second_sum[at] for at in range(4))
+    zs_coarse = Ring(wires, "member_1")
+    zs_coarse.start(lambda to: third_sum.at[zs.me], third_sum)
+    ring_b.finish()
     for x in range(4):
         line_b[x] = (
-            half_b[zs.me, x].astype(f32) + sum(near_b[at, x].astype(f32) for at in zs.order())
+            half_b[zs.me, x].astype(f32) + near_b[0, x].astype(f32) + near_b[1, x].astype(f32)
         ).astype(bf16)
     xs_late.start(lambda to: line_b.at[to], far_b)
 
     homing.advance(1, (0, 3))
+    homing.advance(1, (1, 4))
     zs_coarse.finish()
-    third_sum[ys.me] = sum(second_sum[at] for at in range(4))
-    ys.start(lambda to: third_sum.at[ys.me], third_sum)
-    homing.advance(1, (1, 4))
-
-    ys.finish()
     total[octet.me] = sum(third_sum[at] for at in range(4)).astype(bf16)
     octet.start(lambda to: total.at[octet.me], total)
 
     def reconstruct(pair):
         homing.advance(2, pair)
-        lines = jnp.concatenate(
+        found = jnp.concatenate(
             [returned[chunk].astype(f32).reshape(slots, lanes).astype(bf16) for chunk in pair],
             axis=1,
         )
-        lines = jnp.dot(chosen[...], lines, preferred_element_type=f32).astype(bf16)
+        found = jnp.dot(chosen[...], found, preferred_element_type=f32).astype(bf16)
         for at, chunk in enumerate(pair):
-            rec_ref[:, pl.ds(chunk * lanes, lanes)] = lines[:, at * lanes : (at + 1) * lanes]
+            rec_ref[:, pl.ds(chunk * lanes, lanes)] = found[:, at * lanes : (at + 1) * lanes]
 
     reconstruct((2, 5))
     zs_late.finish()
@@ -540,7 +608,7 @@
     split = width // 2
     moved = (chunks, 4, 4, 4, 2, 2 * cells, lanes)
     eighth = (coarse_total // 8, width + lanes)
-    leaves, lands = 2 * 4 + 3 + 9 + 2, 2 * 4 * chunks + 3 + 9 + 8
+    leaves, lands = 2 * 4 + 3 + 7 + 2 + 4, 2 * 4 * chunks + 3 + 7 + 8 + 6
     f32, bf16 = jnp.float32, jnp.bfloat16
     vmem = pl.BlockSpec(memory_space=pltpu.VMEM)
     hbm = pl.BlockSpec(memory_space=pltpu.HBM)
@@ -558,6 +626,11 @@
         + [
             pltpu.VMEM((chunks + 1, slots, lanes), f32),
             pltpu.VMEM((chunks, slots, lanes), f32),
+            pltpu.VMEM((cells, 2 * 128, width + lanes), bf16),
+            pltpu.VMEM((cells, fine, 2 * 128), f32),
+            pltpu.VMEM((fine_total, lanes), f32),
+            pltpu.VMEM((fine_total, lanes), f32),
+            pltpu.VMEM((cells, 2 * 128, fine), bf16),
             pltpu.VMEM((cells, fine, 2 * 128), bf16),
             pltpu.VMEM((fine_total, width + lanes), bf16),
             pltpu.VMEM((row_count, slots), bf16),
@@ -565,7 +638,9 @@
             pltpu.VMEM((4, 4, mid_dev, width), bf16),
             pltpu.VMEM((4, 4, mid_dev, width), bf16),
         ]
-        + [pltpu.VMEM((4, 4, mid_dev, split), bf16)] * 4
+        + [pltpu.VMEM((4, 4, mid_dev, split), bf16)] * 2
+        + [pltpu.VMEM((2, 4, mid_dev, split), bf16)] * 2
+        + [pltpu.VMEM((2, 2, mid_dev, split), bf16)] * 2
         + [pltpu.VMEM((4, mid_dev, split), bf16)] * 4
         + [pltpu.VMEM((4, 4, 1, lanes), f32)] * 4
         + [pltpu.VMEM((4, 1, lanes), f32)] * 2

time: 71.8 us -> 69.3 us (0.965)
  Pallas kernels: 70.9 us -> 68.3 us
    pallas_call x1, Pallas kernels: 68.8 us -> 66.2 us  [shards(): pl.pallas_call(step_kernel, out_shape=(pltpu.VMEM((fine_total, width), f3...]
where the time goes in v5:
time: 69.3 us; the launch traced here: 69.1 us
  Pallas kernels  68.3 us (99%)
  between operations  0.8 us (1%)
    pallas_call x1, Pallas kernels, shards(): pl.pallas_call(step_kernel, out_shape=(pltpu.VMEM((fine_total, width), f3...  66.2 us
    pallas_call x1, Pallas kernels, shards(): pl.pallas_call(put_out_kernel, out_shape=tuple((jax.ShapeDtypeStruct(one....  2.08 us

profile of v5, /device:TPU:1, one launch (start us, length us, event | category | flops | bytes accessed | tf_op | source)
XLA Modules:
  0.0 69.1 jit_solution(3460081981553602356)
XLA Ops:
  0.6 66.2 %lloyd_step.1 = (f32[1024,768]{1,0:T(8,128)S(1)}, f32[64,768]{1,0:T(8,128)S(1)}, f32[64,768]{1,0:T(8,128)S(1)}, bf16[512,768]{1,0:T(8,128)(2,1)S(1)}) custom-call(bf16[512,768]{1,0:T(8,128)(2,1)} %samples_in.1, s32[1,512]{1,0:T(1,128)} %bitcast.4, bf16[1024,768]{1,0:T(8,128)(2,1)} %fine_in.1, f32[4]{0:T(128)} %sharp_ref.1, s32[1,1024]{1,0:T(1,128)} %bitcast.3, ...), custom_call_target="tpu_custom_call" | custom-call | tf_op jit(solution)/shard_map/lloyd_step/pallas_call | solution.py:615
  66.9 2.1 %put_out.1 = (f32[1024,768]{1,0:T(8,128)}, f32[64,768]{1,0:T(8,128)}, f32[64,768]{1,0:T(8,128)}, bf16[512,768]{1,0:T(8,128)(2,1)}) custom-call(f32[1024,768]{1,0:T(8,128)S(1)} %get-tuple-element.8.refs_0_, f32[64,768]{1,0:T(8,128)S(1)} %get-tuple-element.9.refs_1_, f32[64,768]{1,0:T(8,128)S(1)} %get-tuple-element.10.refs_2_, ...), custom_call_target="tpu_custom_call" | custom-call | tf_op jit(solution)/shard_map/put_out/pallas_call | solution.py:677

commit v6 on v5

--- a/solution.py
+++ b/solution.py
@@ -529,8 +529,6 @@
         ).astype(bf16)
         line_m[z] = half_m[xs.me, z] + sum(near_m[at, z] for at in xs.order())
     zs_late, zs_m, xs_late = Ring(wires, "member_1"), Ring(wires, "member_1"), Ring(wires, "member_0")
-    zs_late.start(lambda to: line_a.at[to], far_a)
-    zs_m.start(lambda to: line_m.at[to], far_m)
 
     homing.advance(1, (2, 5))
     ys.finish()
@@ -545,6 +543,8 @@
     xs_late.start(lambda to: line_b.at[to], far_b)
 
     homing.advance(1, (0, 3))
+    zs_late.start(lambda to: line_a.at[to], far_a)
+    zs_m.start(lambda to: line_m.at[to], far_m)
     homing.advance(1, (1, 4))
     zs_coarse.finish()
     total[octet.me] = sum(third_sum[at] for at in range(4)).astype(bf16)

time: 69.3 us -> 68.9 us (level)
  no operation moved by 1% of the time
where the time goes in v6:
time: 68.9 us; the launch traced here: 68.6 us
  Pallas kernels  67.8 us (98%)
  between operations  0.8 us (1%)
    pallas_call x1, Pallas kernels, shards(): pl.pallas_call(step_kernel, out_shape=(pltpu.VMEM((fine_total, width), f3...  65.7 us
    pallas_call x1, Pallas kernels, shards(): pl.pallas_call(put_out_kernel, out_shape=tuple((jax.ShapeDtypeStruct(one....  2.08 us

profile of v6, /device:TPU:1, one launch (start us, length us, event | category | flops | bytes accessed | tf_op | source)
XLA Modules:
  0.0 68.6 jit_solution(8097664311759482978)
XLA Ops:
  0.6 65.7 %lloyd_step.1 = (f32[1024,768]{1,0:T(8,128)S(1)}, f32[64,768]{1,0:T(8,128)S(1)}, f32[64,768]{1,0:T(8,128)S(1)}, bf16[512,768]{1,0:T(8,128)(2,1)S(1)}) custom-call(bf16[512,768]{1,0:T(8,128)(2,1)} %samples_in.1, s32[1,512]{1,0:T(1,128)} %bitcast.4, bf16[1024,768]{1,0:T(8,128)(2,1)} %fine_in.1, f32[4]{0:T(128)} %sharp_ref.1, s32[1,1024]{1,0:T(1,128)} %bitcast.3, ...), custom_call_target="tpu_custom_call" | custom-call | tf_op jit(solution)/shard_map/lloyd_step/pallas_call | solution.py:615
  66.3 2.1 %put_out.1 = (f32[1024,768]{1,0:T(8,128)}, f32[64,768]{1,0:T(8,128)}, f32[64,768]{1,0:T(8,128)}, bf16[512,768]{1,0:T(8,128)(2,1)}) custom-call(f32[1024,768]{1,0:T(8,128)S(1)} %get-tuple-element.8.refs_0_, f32[64,768]{1,0:T(8,128)S(1)} %get-tuple-element.9.refs_1_, f32[64,768]{1,0:T(8,128)S(1)} %get-tuple-element.10.refs_2_, ...), custom_call_target="tpu_custom_call" | custom-call | tf_op jit(solution)/shard_map/put_out/pallas_call | solution.py:677
